TPU v7x, 128 devices: a whole 4x4x4 slice. The times are simulated.
128 devices in a mesh: dp: 16 (over z, y), tp: 8 (over x, core).
Axes of the slice: x: 4, y: 4, z: 4, core: 2. Of those that a mesh axis runs over, the one named last changes fastest.
Arguments:
- hidden: bfloat16 [2048, 128, 768], P('dp')
- positions: int32 [2048, 20], P('dp')
- labels: int32 [2048, 20], P('dp')
- weights: float32 [2048, 20], P('dp')
- w_t: bfloat16 [768, 768], replicated
- b_t: float32 [768], replicated
- gamma: float32 [768], replicated
- beta: float32 [768], replicated
- embed: bfloat16 [30592, 768], P('tp')
- out_bias: float32 [30592], P('tp')
Outputs:
- output 1: float32 [], replicated
- output 2: bfloat16 [2048, 128, 768], P('dp')
- output 3: float32 [768, 768], replicated
- output 4: float32 [768], replicated
- output 5: float32 [768], replicated
- output 6: float32 [768], replicated
- output 7: float32 [30592, 768], P('tp')
- output 8: float32 [30592], P('tp')
All inputs are finite; a program needn't handle non-finite values.
Results may differ from a plain program's by a relative error of at most 0.001.
Values sent between devices are 32-bit elements.
A program may use at most 1 GiB of HBM per device.

v0:
```python
import jax
import jax.numpy as jnp
from jax import lax
from jax.sharding import PartitionSpec as P

LN_EPS = 1e-12
LOSS_EPS = 1e-5


def gelu_norm(pre_act, gamma, beta):
    activated = jax.nn.gelu(pre_act, approximate=False)
    mean_val = jnp.mean(activated, axis=-1, keepdims=True)
    centered = activated - mean_val
    variance = jnp.mean(centered * centered, axis=-1, keepdims=True)
    return centered * lax.rsqrt(variance + LN_EPS) * gamma + beta


def solution(mesh):
    def local_step(hidden, positions, labels, weights, w_t, b_t, gamma, beta, embed, out_bias):
        batch, seq_len, width = hidden.shape
        max_pred = positions.shape[1]
        shard_vocab = embed.shape[0]
        pos_hot = (positions[:, :, None] == jnp.arange(seq_len, dtype=jnp.int32)[None, None, :]).astype(jnp.bfloat16)
        picked = jnp.einsum("bps,bsd->bpd", pos_hot, hidden, preferred_element_type=jnp.float32).astype(jnp.bfloat16)
        tok_rows = picked.reshape(batch * max_pred, width)
        pre_act = jnp.dot(tok_rows, w_t, preferred_element_type=jnp.float32) + b_t
        normed, norm_vjp = jax.vjp(gelu_norm, pre_act, gamma, beta)
        t_bf = normed.astype(jnp.bfloat16)
        logits = jnp.einsum("nd,vd->nv", t_bf, embed, preferred_element_type=jnp.float32) + out_bias
        row_max = lax.pmax(jnp.max(logits, axis=1), "tp")
        shifted = jnp.exp(logits - row_max[:, None])
        sum_exp = lax.psum(jnp.sum(shifted, axis=1), "tp")
        local_lab = labels.reshape(-1) - lax.axis_index("tp") * shard_vocab
        lab_hot = local_lab[:, None] == jnp.arange(shard_vocab, dtype=jnp.int32)[None, :]
        target_logit = lax.psum(jnp.sum(jnp.where(lab_hot, logits, 0.0), axis=1), "tp")
        flat_w = weights.reshape(-1)
        denom = lax.psum(jnp.sum(flat_w), "dp") + LOSS_EPS
        log_norm = jnp.log(sum_exp) + row_max
        loss = lax.psum(jnp.sum(flat_w * (log_norm - target_logit)), "dp") / denom
        soft_probs = shifted * (1.0 / sum_exp)[:, None]
        d_logits = jnp.where(lab_hot, soft_probs - 1.0, soft_probs) * (flat_w / denom)[:, None]
        dz_bf = d_logits.astype(jnp.bfloat16)
        d_embed = lax.psum(jnp.einsum("nv,nd->vd", dz_bf, t_bf, preferred_element_type=jnp.float32), "dp")
        d_out_bias = lax.psum(jnp.sum(d_logits, axis=0), "dp")
        d_normed = lax.psum(jnp.einsum("nv,vd->nd", dz_bf, embed, preferred_element_type=jnp.float32), "tp")
        d_pre, d_gamma, d_beta = norm_vjp(d_normed)
        d_pre_bf = d_pre.astype(jnp.bfloat16)
        d_w_t = lax.psum(jnp.einsum("nd,ne->de", tok_rows, d_pre_bf, preferred_element_type=jnp.float32), "dp")
        d_b_t = lax.psum(jnp.sum(d_pre, axis=0), "dp")
        d_gamma = lax.psum(d_gamma, "dp")
        d_beta = lax.psum(d_beta, "dp")
        d_rows = jnp.einsum("ne,de->nd", d_pre_bf, w_t, preferred_element_type=jnp.float32).astype(jnp.bfloat16)
        d_hidden = jnp.einsum("bps,bpd->bsd", pos_hot, d_rows.reshape(batch, max_pred, width), preferred_element_type=jnp.float32).astype(jnp.bfloat16)
        return loss, d_hidden, d_w_t, d_b_t, d_gamma, d_beta, d_embed, d_out_bias

    in_specs = (P("dp", None, None), P("dp", None), P("dp", None), P("dp", None), P(None, None), P(None), P(None), P(None), P("tp", None), P("tp"))
    out_specs = (P(), P("dp", None, None), P(None, None), P(None), P(None), P(None), P("tp", None), P("tp"))
    return jax.shard_map(local_step, mesh=mesh, in_specs=in_specs, out_specs=out_specs, check_vma=False)
```

profile of v0, /device:TPU:1, one launch (start us, length us, event | category | flops | bytes accessed | tf_op | source)
XLA Modules:
  0.0 581.7 jit_solution(3946794819739956078)
XLA Ops:
  7.2 0.9 copy.20
  8.1 1.3 reduce_sum.129
  9.4 36.1 %psum.80 = f32[]{:T(128)} all-reduce(f32[]{:T(128)} %reduce_sum.129), channel_id=1, replica_groups=mesh['dp'=16,'tp'=8] {'dp'}, use_global_device_ids=true, to_apply=%region_11.12 | all-reduce | flops 1 | bytes 8 | tf_op jit(solution)/shard_map/psum | solution.py:37
  45.6 0.7 broadcast_subtract_fusion
  46.5 0.8 copy.21
  47.4 12.2 %convolution_convert_fusion.2 = bf16[128,20,768]{2,1,0:T(8,128)(2,1)} fusion(bf16[128,128,768]{2,1,0:T(8,128)(2,1)} %param.10, s32[128,20]{1,0:T(8,128)S(1)} %copy.21), kind=kOutput, calls=%fused_computation.34 | convolution fusion | flops 505610240 | bytes 29108224 | tf_op jit(solution)/shard_map/bps,bsd->bpd/dot_general | solution.py:24
  59.7 6.9 %reshape.76 = bf16[2560,768]{1,0:T(8,128)(2,1)} reshape(bf16[128,20,768]{2,1,0:T(8,128)(2,1)} %convolution_convert_fusion.2) | data formatting | bytes 7864320 | tf_op jit(solution)/shard_map/reshape | solution.py:25
  66.6 24.2 %fusion.21 = (f32[2560]{0:T(1024)S(1)}, f32[2560,768]{0,1:T(8,128)S(1)}, f32[2560,768]{0,1:T(8,128)}, f32[2560,768]{0,1:T(8,128)}) fusion(f32[768]{0:T(1024)S(1)} %copy-done.8, bf16[2560,768]{1,0:T(8,128)(2,1)} %reshape.76, bf16[768,768]{1,0:T(8,128)(2,1)S(1)} %copy-done), kind=kOutput, calls=%fused_computation.54 | convolution fusion | flops 3149657600 | bytes 28718080 | tf_op jit(solution)/shard_map/dot_general | solution.py:26
  90.8 0.9 multiply_reduce_fusion.2
  91.7 25.0 %add_reduce_fusion = (f32[2560]{0:T(1024)S(1)}, f32[2560,3824]{0,1:T(8,128)}) fusion(f32[3824]{0:T(1024)S(1)} %copy-done.6, bf16[3824,768]{1,0:T(8,128)(2,1)} %param.18, f32[2560,768]{0,1:T(8,128)S(1)} %get-tuple-element.24, f32[768]{0:T(1024)S(1)} %copy-done.9, f32[768]{0:T(1024)S(1)} %copy-done.7, f32[2560]{0:T(1024)S(1)} %fusion.16, ...), kind=kOutput, calls=%fused_computation.6 | convolution fusion | flops 15065987072 | bytes 52947904 | tf_op jit(solution)/shard_map/nd,vd->nv/dot_general | solution.py:29
  116.7 27.9 %pmax.7 = f32[2560]{0:T(1024)S(1)} all-reduce(f32[2560]{0:T(1024)S(1)} %get-tuple-element.28), channel_id=1, replica_groups=mesh['dp'=16,'tp'=8] {'tp'}, use_global_device_ids=true, to_apply=%region_3.0 | all-reduce | flops 2560 | bytes 20480 | tf_op jit(solution)/shard_map/pmax | solution.py:30
  144.6 16.7 %fusion.1 = f32[2560]{0:T(1024)S(1)} fusion(f32[2560,3824]{0,1:T(8,128)} %get-tuple-element.29, f32[2560]{0:T(1024)S(1)} %pmax.7, f32[3824]{0:T(1024)S(1)} %copy-done.6), kind=kLoop, calls=%fused_computation.5 | loop fusion | flops 29365760 | bytes 39193536 | tf_op jit(solution)/shard_map/reduce_sum | solution.py:32
  161.3 23.8 %psum.77 = f32[2560]{0:T(1024)S(1)} all-reduce(f32[2560]{0:T(1024)S(1)} %fusion.1), channel_id=1, replica_groups=mesh['dp'=16,'tp'=8] {'tp'}, use_global_device_ids=true, to_apply=%region_5.0 | all-reduce | flops 2560 | bytes 20480 | tf_op jit(solution)/shard_map/psum | solution.py:32
  185.8 30.1 %fusion.2 = (f32[3824]{0:T(1024)S(1)}, f32[2560]{0:T(1024)S(1)}, bf16[2560,3824]{0,1:T(8,128)(2,1)}) fusion(f32[2560,3824]{0,1:T(8,128)} %get-tuple-element.29, f32[2560]{0:T(1024)S(1)} %broadcast_divide_fusion, f32[2560]{0:T(1024)S(1)} %broadcast_divide_fusion.1, s32[2560]{0:T(1024)S(1)} %sub.42, f32[2560]{0:T(1024)S(1)} %pmax.7, f32[3824]{0:T(1024)S(1)} %copy-done.6), kind=kLoop, calls=%fused_computation.7 | loop fusion | flops 107677456 | bytes 58818432 | tf_op jit(solution)/shard_map/reduce_sum | solution.py:44
  215.9 23.5 %fusion.23 = f32[2560,768]{0,1:T(8,128)} fusion(bf16[2560,3824]{0,1:T(8,128)(2,1)} %get-tuple-element.26, bf16[3824,768]{1,0:T(8,128)(2,1)} %param.18), kind=kOutput, calls=%fused_computation.55 | convolution fusion | flops 15036579840 | bytes 33316864 | tf_op jit(solution)/shard_map/nv,vd->nd/dot_general | solution.py:45
  239.4 23.8 %fusion.17 = f32[3824,768]{1,0:T(8,128)} fusion(bf16[2560,3824]{0,1:T(8,128)(2,1)} %get-tuple-element.26, f32[2560,768]{0,1:T(8,128)} %copy-done.1, f32[768]{0:T(1024)S(1)} %copy-done.9, f32[768]{0:T(1024)S(1)} %copy-done.7, f32[2560]{0:T(1024)S(1)} %fusion.16, f32[2560]{0:T(1024)S(1)} %broadcast_multiply_fusion), kind=kOutput, calls=%fused_computation.50 | convolution fusion | flops 15046410240 | bytes 39217152 | tf_op jit(solution)/shard_map/nv,nd->vd/dot_general | solution.py:43
  263.3 71.2 %all-reduce.5.cloned.1.call-done = f32[2560,768]{0,1:T(8,128)} async-done(((f32[2560,768]{0,1:T(8,128)}), f32[2560,768]{0,1:T(8,128)}) %all-reduce.5.cloned.1.call-update) | async-done | bytes 7864336 | tf_op jit(solution)/shard_map/psum | solution.py:45
  334.4 6.8 %fusion.19 = (f32[768]{0:T(1024)S(1)}, f32[2560]{0:T(1024)S(1)}) fusion(f32[2560,768]{0,1:T(8,128)} %all-reduce.5.cloned.1.call-done, f32[768]{0:T(1024)S(1)} %copy-done.7, f32[2560,768]{0,1:T(8,128)} %copy-done.1, f32[2560]{0:T(1024)S(1)} %broadcast_multiply_fusion), kind=kLoop, calls=%fused_computation.52 | loop fusion | flops 9827072 | bytes 15755264 | tf_op jit(solution)/shard_map/transpose(jvp())/reduce_sum | solution.py:15
  341.3 0.9 copy-done.2
  342.2 6.7 %multiply_reduce_fusion = (f32[768]{0:T(1024)S(1)}, f32[2560]{0:T(1024)S(1)}) fusion(f32[2560,768]{0,1:T(8,128)S(1)} %copy-done.2, f32[2560,768]{0,1:T(8,128)} %copy-done.1, f32[2560]{0:T(1024)S(1)} %fusion.16, f32[2560]{0:T(1024)S(1)} %broadcast_multiply_fusion, f32[2560]{0:T(1024)S(1)} %multiply_multiply_fusion.6, f32[768]{0:T(1024)S(1)} %copy-done.7), kind=kLoop, calls=%fused_computation.13 | loop fusion | flops 19657472 | bytes 15775744 | tf_op jit(solution)/shard_map/transpose(jvp())/reduce_sum | solution.py:15
  348.9 0.3 slice-done.3
  349.2 10.4 %fusion.20 = (f32[768]{0:T(1024)S(1)}, bf16[2560,768]{0,1:T(8,128)(2,1)}) fusion(f32[2560,768]{0,1:T(8,128)S(1)} %bitcast.15, f32[2560]{0:T(1024)S(1)} %negate_multiply_fusion.1, f32[2560]{0:T(1024)S(1)} %multiply_multiply_fusion.6, f32[2560,768]{0,1:T(8,128)S(1)} %bitcast.13, f32[2560]{0:T(1024)S(1)} %broadcast_multiply_fusion, f32[2560]{0:T(1024)S(1)} %fusion.16, ...), kind=kLoop, calls=%fused_computation.53 | loop fusion | flops 45219072 | bytes 35439616 | tf_op jit(solution)/shard_map/reduce_sum | solution.py:49
  359.7 6.8 %fusion.11 = f32[768,768]{1,0:T(8,128)} fusion(bf16[2560,768]{1,0:T(8,128)(2,1)S(1)} %copy-done.3, bf16[2560,768]{0,1:T(8,128)(2,1)} %get-tuple-element.22), kind=kOutput, calls=%fused_computation.35 | convolution fusion | flops 3019898880 | bytes 10223616 | tf_op jit(solution)/shard_map/nd,ne->de/dot_general | solution.py:48
  366.5 21.8 %psum.78 = f32[2560]{0:T(1024)S(1)} all-reduce(f32[2560]{0:T(1024)S(1)} %get-tuple-element.9), channel_id=1, replica_groups=mesh['dp'=16,'tp'=8] {'tp'}, use_global_device_ids=true, to_apply=%region_7.8 | all-reduce | flops 2560 | bytes 20480 | tf_op jit(solution)/shard_map/psum | solution.py:35
  388.2 0.6 multiply_reduce_fusion.3
  388.9 62.8 %all-reduce = (f32[]{:T(128)}, f32[768]{0:T(1024)}, f32[768]{0:T(1024)}, f32[768]{0:T(1024)}, f32[3824]{0:T(1024)}) all-reduce(f32[]{:T(128)} %multiply_reduce_fusion.3, f32[768]{0:T(1024)S(1)} %get-tuple-element.21, f32[768]{0:T(1024)S(1)} %get-tuple-element.10, ...), channel_id=1, replica_groups=mesh['dp'=16,'tp'=8] {'dp'}, use_global_device_ids=true, to_apply=%region_9.10 | all-reduce | flops 6129 | bytes 49032 | tf_op jit(solution)/shard_map/psum | solution.py:39
  452.3 7.3 %convolution_convert_fusion.1 = bf16[2560,768]{1,0:T(8,128)(2,1)} fusion(bf16[768,768]{1,0:T(8,128)(2,1)S(1)} %copy-done, bf16[2560,768]{0,1:T(8,128)(2,1)} %get-tuple-element.22), kind=kOutput, calls=%fused_computation.32 | convolution fusion | flops 3021864960 | bytes 9043968 | tf_op jit(solution)/shard_map/ne,de->nd/dot_general | solution.py:52
  459.5 6.9 %reshape.77 = bf16[128,20,768]{2,1,0:T(8,128)(2,1)} reshape(bf16[2560,768]{1,0:T(8,128)(2,1)} %convolution_convert_fusion.1) | data formatting | bytes 7864320 | tf_op jit(solution)/shard_map/reshape | solution.py:53
  466.5 17.2 %convolution_convert_fusion = bf16[128,128,768]{2,1,0:T(8,128)(2,1)} fusion(bf16[128,20,768]{2,1,0:T(8,128)(2,1)} %reshape.77, s32[128,20]{1,0:T(8,128)S(1)} %copy-done.5), kind=kOutput, calls=%fused_computation.9 | convolution fusion | flops 516227072 | bytes 29108224 | tf_op jit(solution)/shard_map/bps,bpd->bsd/dot_general | solution.py:53
  483.6 77.1 %all-reduce.7.cloned.1.call-done = (f32[768,768]{1,0:T(8,128)}, f32[3824,768]{1,0:T(8,128)}) async-done(((f32[768,768]{1,0:T(8,128)}, f32[3824,768]{1,0:T(8,128)}), (f32[768,768]{1,0:T(8,128)}, f32[3824,768]{1,0:T(8,128)})) %all-reduce.7.cloned.1.call-update) | async-done | bytes 14106640 | tf_op jit(solution)/shard_map/psum | solution.py:48
  560.7 3.2 copy.28
  563.9 9.6 %copy.29 = f32[3824,768]{1,0:T(8,128)} copy(f32[3824,768]{1,0:T(8,128)} %get-tuple-element.38) | data formatting | bytes 23494656
  (41 shorter events, 0.5 us)
Async XLA Ops:
  7.2 59.4 %copy-start = (bf16[768,768]{1,0:T(8,128)(2,1)S(1)}, bf16[768,768]{1,0:T(8,128)(2,1)}, u32[]{:S(2)}) copy-start(bf16[768,768]{1,0:T(8,128)(2,1)} %param.14) | copy-start | bytes 3538948
  7.2 327.3 %all-reduce.5.cloned.1.call-start = ((), (), s32[]{:S(2)}) async-start(), calls=%async_computation | async-start | bytes 15728640 | tf_op jit(solution)/shard_map/psum | solution.py:45
  47.3 12.3 %copy-start.4 = (s32[128,20]{1,0:T(8,128)}, s32[128,20]{1,0:T(8,128)S(1)}, u32[]{:S(2)}) copy-start(s32[128,20]{1,0:T(8,128)S(1)} %copy.21) | copy-start | bytes 30724
  59.7 6.9 %copy-start.8 = (f32[768]{0:T(1024)S(1)}, f32[768]{0:T(1024)}, u32[]{:S(2)}) copy-start(f32[768]{0:T(1024)} %param.15) | copy-start | bytes 9220
  90.7 26.0 %copy-start.1 = (f32[2560,768]{0,1:T(8,128)}, f32[2560,768]{0,1:T(8,128)S(1)}, u32[]{:S(2)}) copy-start(f32[2560,768]{0,1:T(8,128)S(1)} %get-tuple-element.24) | copy-start | bytes 23592964
  90.7 1.0 copy-start.6
  90.7 1.0 copy-start.7
  90.7 1.0 copy-start.9
  239.4 321.3 %all-reduce.7.cloned.1.call-start = ((), (), s32[]{:S(2)}) async-start(), calls=%async_computation.1 | async-start | bytes 28213248 | tf_op jit(solution)/shard_map/psum | solution.py:48
  334.4 7.8 %copy-start.2 = (f32[2560,768]{0,1:T(8,128)S(1)}, f32[2560,768]{0,1:T(8,128)}, u32[]{:S(2)}) copy-start(f32[2560,768]{0,1:T(8,128)} %all-reduce.5.cloned.1.call-done) | copy-start | bytes 23592964
  334.4 14.5 %slice-start = ((s8[7864320]{0:T(1024)(128)(4,1)}), s8[4194304]{0:T(1024)(128)(4,1)S(1)}, s32[]{:S(2)}) async-start(s8[7864320]{0:T(1024)(128)(4,1)} %bitcast.12), calls=%async_computation.2 | async-start | bytes 8388608
  334.4 14.5 %slice-start.2 = ((s8[7864320]{0:T(1024)(128)(4,1)}), s8[4194304]{0:T(1024)(128)(4,1)S(1)}, s32[]{:S(2)}) async-start(s8[7864320]{0:T(1024)(128)(4,1)} %bitcast.14), calls=%async_computation.4 | async-start | bytes 8388608
  342.2 6.7 %slice-start.1 = ((s8[7864320]{0:T(1024)(128)(4,1)}), s8[3670016]{0:T(1024)(128)(4,1)S(1)}, s32[]{:S(2)}) async-start(s8[7864320]{0:T(1024)(128)(4,1)} %bitcast.12), calls=%async_computation.3 | async-start | bytes 7340032
  342.2 7.0 %slice-start.3 = ((s8[7864320]{0:T(1024)(128)(4,1)}), s8[3670016]{0:T(1024)(128)(4,1)S(1)}, s32[]{:S(2)}) async-start(s8[7864320]{0:T(1024)(128)(4,1)} %bitcast.14), calls=%async_computation.5 | async-start | bytes 7340032
  349.2 10.4 %copy-start.3 = (bf16[2560,768]{1,0:T(8,128)(2,1)S(1)}, bf16[2560,768]{1,0:T(8,128)(2,1)}, u32[]{:S(2)}) copy-start(bf16[2560,768]{1,0:T(8,128)(2,1)} %reshape.76) | copy-start | bytes 11796484
  459.5 6.9 %copy-start.5 = (s32[128,20]{1,0:T(8,128)S(1)}, s32[128,20]{1,0:T(8,128)}, u32[]{:S(2)}) copy-start(s32[128,20]{1,0:T(8,128)} %copy-done.4) | copy-start | bytes 30724
Sparse Core Ops, SparseCore 0:
  239.5 94.8 all-reduce.4
  366.6 194.0 all-reduce.6
where the time goes:
time: 590 us; the launch traced here: 582 us
  blocking collectives  172 us (29%)
  waiting for transfers between devices  148 us (25%)
  matrix products  140 us (24%)
  other arithmetic  74.2 us (13%)
  local copies, waits for them, and re-layouts  29.9 us (5%)
  between operations  16.8 us (3%)
    psum x1, waiting for transfers between devices, local_step(): lax.psum(jnp.einsum('nd,ne->de', tok_rows, d_pre_bf, preferred_element_ty...  77.1 us
    psum x1, waiting for transfers between devices, local_step(): lax.psum(jnp.einsum('nv,vd->nd', dz_bf, embed, preferred_element_type=jnp...  71.2 us
    psum x1, blocking collectives, local_step(): loss = lax.psum(jnp.sum(flat_w * (log_norm - target_logit)), 'dp') / denom  62.8 us
    psum x1, blocking collectives, local_step(): denom = lax.psum(jnp.sum(flat_w), 'dp') + LOSS_EPS  36.1 us
    reduce_sum x1, other arithmetic, local_step(): d_out_bias = lax.psum(jnp.sum(d_logits, axis=0), 'dp')  30.1 us
    pmax x1, blocking collectives, local_step(): row_max = lax.pmax(jnp.max(logits, axis=1), 'tp')  27.9 us
    dot_general x1, matrix products, local_step(): jnp.einsum('nd,vd->nv', t_bf, embed, preferred_element_type=jnp.float32)  25 us
    dot_general x1, matrix products, local_step(): pre_act = jnp.dot(tok_rows, w_t, preferred_element_type=jnp.float32) + b_t  24.2 us
  transfers between devices with their start and end apart: 2, of which 2 were waited for; matrix products, arithmetic and copies ran while one was open for 10% of the time, Pallas kernels for 0%

commit v1 on v0

v1 whole, which is shorter than its diff:
```python
import functools

import jax
import jax.numpy as jnp
from jax import lax
from jax.experimental import pallas as pl
from jax.experimental.pallas import tpu as pltpu
from jax.sharding import PartitionSpec as P

F32 = jnp.float32
BF16 = jnp.bfloat16
I32 = jnp.int32
LN_EPS = 1e-12
LOSS_EPS = 1e-5
RSQRT2 = 0.7071067811865476
PAD_BIAS = -3e38
GB = 8
NT = 5
NBUF = 4
VMEM_MAX = 67043328
NCH = 8
NN = (((1,), (0,)), ((), ()))
NTR = (((1,), (1,)), ((), ()))
TN = (((0,), (0,)), ((), ()))


def mm(a, b, dims=NN):
    return lax.dot_general(a, b, dims, preferred_element_type=F32)


LANES = 128
ALL = None
ROWS, COLS = ({"axis": i, "keepdims": True} for i in range(2))
LAB, LIVE, SRC, MAX, SUM, TGT = (slice(i, i + 1) for i in range(6))


class Dims:
    def __init__(self, hidden, positions, embed):
        self.B, self.L, self.D = hidden
        self.P = positions[1]
        self.V = embed[0]
        self.G = self.B // GB
        self.S = GB * self.P
        self.N = self.B * self.P
        self.TT = self.N // NT
        self.BLK = -(-self.V // LANES) * GB
        self.VP = 16 * self.BLK
        self.CH = 2 * self.BLK
        self.NR = self.N // 8
        self.HN, self.HD, self.HB, self.HR = self.N // 2, self.D // 2, self.BLK // 2, self.NR // 2
        self.WR = self.D // 8
        self.WP = self.WR // 4
        self.CL = -(-self.CH // LANES) * LANES


def cuts(n):
    return [slice(i, min(i + LANES, n)) for i in range(0, n, LANES)]


def row_of(ref):
    return jnp.concatenate([ref[slice(i, i + 1), :] for i in range(ref.shape[0])], axis=1)


def forward_kernel(d, h_hbm, idx_ref, lab_ref, w_ref, wt_ref, bt_ref, gm_ref, be_ref, e_hbm, bias_ref,
                   h_out, t_out, z_out, meta_out, col_out, e_out, cnt_out,
                   hin, hb, tb, ub, eb, bcol, zb, col, meta, keys, cntv, cnt, par3, hsem, esem, zsem, osem):
    rows_g = GB * d.L
    tail = d.V - (NCH - 1) * d.CH

    def h_copy(g, slot):
        return pltpu.make_async_copy(h_hbm.at[pl.ds(g * rows_g, rows_g)], hin.at[slot], hsem.at[slot])

    def e_copy(c):
        n = d.CH if c < NCH - 1 else tail
        return pltpu.make_async_copy(e_hbm.at[pl.ds(c * d.CH, n)], eb.at[pl.ds(c * d.CH, n)], esem.at[c])

    for g in range(NBUF):
        h_copy(g, g).start()
    for c in range(NCH):
        e_copy(c).start()

    cntv[...] = jnp.broadcast_to(jnp.sum(w_ref[...], **ROWS), cntv.shape).astype(I32)
    to_smem = pltpu.make_async_copy(cntv, cnt, osem.at[5])
    to_smem.start()
    outs = [pltpu.make_async_copy(a, b, osem.at[i])
            for i, (a, b) in enumerate(((hb, h_out), (col, col_out), (eb, e_out), (tb, t_out), (meta, meta_out)))]
    outs.append(pltpu.make_async_copy(cntv, cnt_out, osem.at[6]))
    outs[5].start()

    key = lab_ref[...] * 2048 + idx_ref[...] + 1
    keys[...] = jnp.concatenate([key, jnp.zeros((LANES - d.P, d.B), I32)], axis=0).T
    for i, ref in enumerate((bt_ref, gm_ref, be_ref)):
        par3[slice(i, i + 1), :] = row_of(ref)
    hb[...] = jnp.zeros_like(hb)
    tb[...] = jnp.zeros_like(tb)
    col[...] = jnp.zeros_like(col)
    if tail < d.CH:
        eb[d.V:, :] = jnp.zeros((d.VP - d.V, d.D), BF16)
    one_row = lax.broadcasted_iota(I32, (8, d.TT), 0) == 4
    for n in range(NT):
        meta[n] = jnp.where(one_row, 1.0, 0.0)
    for i, rows in enumerate(cuts(d.VP)):
        bcol[rows, :] = jnp.broadcast_to(bias_ref[slice(i, i + 1), :], (LANES, LANES)).T
    to_smem.wait()

    lane = lax.broadcasted_iota(I32, (1, LANES), 1)
    r_iota = lax.broadcasted_iota(I32, (d.S, LANES), 0)
    p_iota = lax.broadcasted_iota(I32, (1, LANES), 1)
    src_iota = lax.broadcasted_iota(I32, (d.S, rows_g), 1)

    def group(g, o):
        slot = lax.rem(g, NBUF)
        off = jnp.int32(0)
        key = jnp.zeros((d.S, LANES), I32)
        for j in range(GB):
            b = g * GB + j
            n_j = cnt[0, b]
            rank = jnp.where(p_iota < n_j, p_iota + off, -1)
            key = key + jnp.where(r_iota == rank, keys[pl.ds(b, 1), :] + j * d.L, 0)
            off = off + n_j
        src = jnp.sum((key & 2047).astype(F32), **COLS)
        lab = jnp.sum((key >> 11).astype(F32), **COLS)
        hot = (src_iota == src.astype(I32) - 1).astype(BF16)
        h_copy(g, slot).wait()
        o = pl.multiple_of(o, 16)
        hb[pl.ds(o, d.S), :] = mm(hot, hin[slot]).astype(BF16)
        live = (src > 0).astype(F32)
        col[pl.ds(o, d.S), :] = jnp.where(lane == 0, lab, jnp.where(lane == 1, live, src - 1))

        @pl.when(g + NBUF < d.G)
        def _():
            h_copy(g + NBUF, slot).start()

        return o + ((off + 15) // 16) * 16

    used = lax.fori_loop(0, d.G, group, jnp.int32(0))
    tiles = (used + d.TT - 1) // d.TT
    outs[0].start()
    outs[1].start()
    for c in range(NCH):
        e_copy(c).wait()
    outs[2].start()

    base_v = lax.axis_index("tp") * d.V
    sub = lax.broadcasted_iota(I32, (8, d.TT), 0)
    rb = min(128, d.TT)

    def z_copy(n, c):
        return pltpu.make_async_copy(zb.at[lax.rem(n, 2), c], z_out.at[n, pl.ds(c * d.CH, d.CH)],
                                     zsem.at[lax.rem(n, 2), c])

    def tile(n, carry):
        par = lax.rem(n, 2)
        base = pl.multiple_of(n * d.TT, d.TT)

        @pl.when(n >= 2)
        def _():
            for c in range(NCH):
                z_copy(n, c).wait()

        ub[...] = mm(hb[pl.ds(base, d.TT), :], wt_ref[...]) + par3[LAB, :]

        def norm(i, carry):
            r = pl.multiple_of(i * rb, rb)
            u = ub[pl.ds(r, rb), :]
            a = 0.5 * u * (1.0 + lax.erf(u * RSQRT2))
            ctr = a - jnp.mean(a, **COLS)
            var = jnp.mean(ctr * ctr, **COLS)
            t = ctr * lax.rsqrt(var + LN_EPS) * par3[LIVE, :] + par3[SRC, :]
            tb[pl.ds(base + r, rb), :] = t.astype(BF16)
            return carry

        lax.fori_loop(0, d.TT // rb, norm, 0)
        for cols in cuts(d.TT):
            blk = col[pl.ds(base + cols.start, LANES), :].T
            meta[n, :3, cols] = blk[:3, :]

        t_n = tb[pl.ds(base, d.TT), :]
        lab = meta[n, LAB, :].astype(I32) - base_v
        lab8 = jnp.broadcast_to(jnp.where(lab < d.V, lab, -1), (8, d.TT))
        m8 = jnp.full((8, d.TT), -jnp.inf, F32)
        s8 = jnp.zeros((8, d.TT), F32)
        t8 = jnp.zeros((8, d.TT), F32)
        reps = d.TT // LANES

        def product(c):
            z = mm(eb[c * d.CH:(c + 1) * d.CH, :], t_n, NTR)
            b = bcol[c * d.CH:(c + 1) * d.CH, :]
            z = z + jnp.concatenate([b] * reps, axis=1)
            zb[par, c] = z
            mx = jnp.max(z.reshape(d.CH // 8, 8, d.TT), axis=0)
            return jnp.broadcast_to(jnp.max(mx, **ROWS), (8, d.TT))

        nxt = product(0)
        for c in range(NCH):
            z_copy(n, c).start()
            mx = jnp.maximum(m8, nxt)
            if c + 1 < NCH:
                nxt = product(c + 1)
            s8 = s8 * jnp.exp(m8 - mx)
            m8 = mx
            for i in range(d.CH // 8):
                zz = zb[par, c, i * 8:(i + 1) * 8, :]
                s8 = s8 + jnp.exp(zz - m8)
                t8 = t8 + jnp.where(sub + (c * d.CH + i * 8) == lab8, zz, 0.0)
        meta[n, MAX, :] = m8[LAB, :]
        meta[n, SUM, :] = jnp.sum(s8, **ROWS)
        meta[n, TGT, :] = jnp.sum(t8, **ROWS)
        return carry

    lax.fori_loop(0, tiles, tile, 0)
    outs[3].start()
    outs[4].start()

    def drain(n, carry):
        for c in range(NCH):
            z_copy(n, c).wait()
        return carry

    lax.fori_loop(jnp.maximum(tiles - 2, 0), tiles, drain, 0)
    for cp in outs:
        cp.wait()


def forward(d, h2, idx, lab, w, w_t, bt, gm, be, embed, bias):
    any_ = pl.BlockSpec(memory_space=pl.ANY)
    vm = pl.BlockSpec(memory_space=pltpu.VMEM)
    sd = jax.ShapeDtypeStruct
    dma = pltpu.SemaphoreType.DMA
    return pl.pallas_call(
        functools.partial(forward_kernel, d),
        out_shape=(sd((d.N, d.D), BF16), sd((d.N, d.D), BF16), sd((NT, d.VP, d.TT), F32), sd((NT, 8, d.TT), F32),
                   sd((d.N, LANES), F32), sd((d.VP, d.D), BF16), sd((8, d.B), I32)),
        in_specs=[any_, vm, vm, vm, vm, vm, vm, vm, any_, vm],
        out_specs=(any_,) * 7,
        scratch_shapes=[
            pltpu.VMEM((NBUF, GB * d.L, d.D), BF16),
            pltpu.VMEM((d.N, d.D), BF16),
            pltpu.VMEM((d.N, d.D), BF16),
            pltpu.VMEM((d.TT, d.D), F32),
            pltpu.VMEM((d.VP, d.D), BF16),
            pltpu.VMEM((d.VP, LANES), F32),
            pltpu.VMEM((2, NCH, d.CH, d.TT), F32),
            pltpu.VMEM((d.N, LANES), F32),
            pltpu.VMEM((NT, 8, d.TT), F32),
            pltpu.VMEM((d.B, LANES), I32),
            pltpu.VMEM((8, d.B), I32),
            pltpu.SMEM((8, d.B), I32),
            pltpu.VMEM((8, d.D), F32),
            dma((NBUF,)), dma((NCH,)), dma((2, NCH)), dma((7,)),
        ],
        compiler_params=pltpu.CompilerParams(vmem_limit_bytes=VMEM_MAX),
        name="mlm_forward",
    )(h2, idx, lab, w, w_t, bt, gm, be, embed, bias)


MESH = pl.DeviceIdType.MESH
RING = (1, 2, 3)
NSEM = 128
ORDER = ((2, 0), (2, 1), (1, 1), (3, 0), (1, 0), (3, 1), (0, 0), (0, 1))
FINISH = (0, 3, 1, 2)


def train_kernel(d, t_hbm, h_hbm, z_hbm, meta, e_hbm, wt_ref, bt_ref, gm_ref, be_ref,
                 de_out, dh_out, dwt_out, vec_out, dbo_out,
                 tb, eb, zb, dzb, dt, de, fm, fp, r2a, r2b, f2m, f2p, dr, xa, xb, xm, xp,
                 ub, dub, hown, wr, wxa, wxb, wxm, wxp, wp, wq, wag, srecv, comb, dacc, vb, vby, vbz,
                 dnp, dnq, vec, vect, vecy, vecz, lsem, esem, zsem, osem, ss, rs):
    dp = lax.axis_index("dp")
    tp = lax.axis_index("tp")
    zc, yc = dp // 4, lax.rem(dp, 4)
    x, core = tp // 2, lax.rem(tp, 2)
    other = 1 - core
    pm, qm = 1 + 3 * core, 4 - 3 * core
    p = yc + core * (zc - yc)
    q = zc + core * (yc - zc)
    N, D, CH, BLK, TT, NR = d.N, d.D, d.CH, d.BLK, d.TT, d.NR
    HN, HD, WR, WP = d.HN, d.HD, d.WR, d.WP

    def rem4(v):
        return lax.rem(v + 4, 4)

    def rem8(v):
        return lax.rem(v + 8, 8)

    def at_p(r):
        return {"dp": rem4(p + r) * pm + q * qm}

    def at_q(r):
        return {"dp": p * pm + rem4(q + r) * qm}

    def at_y(r):
        return {"dp": zc * 4 + rem4(yc + r)}

    def at_z(r):
        return {"dp": rem4(zc + r) * 4 + yc}

    def at_x(r):
        return {"tp": rem4(x + r) * 2 + core}

    def at_t(r):
        return {"tp": rem8(tp + r)}

    sib = {"tp": x * 2 + other}

    def al(v, m=8):
        return pl.multiple_of(v, m)

    listed = []

    def link(src, dst, dev):
        i = len(listed)
        listed.append(pltpu.make_async_remote_copy(src_ref=src, dst_ref=dst, send_sem=ss.at[i], recv_sem=rs.at[i],
                                                   device_id=dev, device_id_type=MESH))
        return i

    def send(src, dst, dev):
        i = link(src, dst, dev)
        listed[i].start()
        return i

    def got(dst, i):
        pltpu.make_async_remote_copy(src_ref=dst, dst_ref=dst, send_sem=ss.at[i], recv_sem=rs.at[i],
                                     device_id=sib, device_id_type=MESH).wait_recv()

    def share(buf, own, at):
        return [send(buf.at[own], buf.at[own], at(r)) for r in RING]

    def shared(buf, own, ids):
        for r, i in zip(RING, ids):
            got(buf.at[rem4(own - r)], i)
        return buf[0] + buf[1] + buf[2] + buf[3]

    def half(ref, h):
        n = ref.shape[0] // 2
        return ref.at[pl.ds(h * n, n)]

    def add(dst, srcs):
        nr = dst.shape[0]
        step = max(s for s in (8, 24, 40) if nr % s == 0)

        def body(i, carry):
            rows = pl.ds(al(i * step), step)
            v = dst[rows, :]
            for s in srcs:
                v = v + s[rows, :]
            dst[rows, :] = v
            return carry

        lax.fori_loop(0, nr // step, body, 0)

    class Scatter:
        def __init__(self, blk, a, b, m, pp, at):
            self.blk, self.a, self.b, self.m, self.pp, self.at = blk, a, b, m, pp, at

        def begin(self):
            blk, at = self.blk, self.at
            self.ids = [send(blk(2, 0), self.a, at(1)), send(blk(2, 1), self.b, at(3)),
                        send(blk(1, 1), half(self.m, 1), at(1)), send(blk(3, 0), half(self.pp, 0), at(3))]

        def middle(self):
            blk, at = self.blk, self.at
            got(self.a, self.ids[0])
            add(blk(1, 0), [self.a])
            self.ids.append(send(blk(1, 0), half(self.m, 0), at(1)))
            got(self.b, self.ids[1])
            add(blk(3, 1), [self.b])
            self.ids.append(send(blk(3, 1), half(self.pp, 1), at(3)))

        def end(self):
            ids = self.ids
            got(half(self.m, 1), ids[2])
            got(half(self.pp, 0), ids[3])
            got(half(self.m, 0), ids[4])
            got(half(self.pp, 1), ids[5])

    class Gather:
        def __init__(self, row, at, to_sib=None):
            self.row, self.at, self.to_sib, self.sib_ids = row, at, to_sib, []

        def pass_on(self, r, src=None):
            if self.to_sib is not None:
                src = self.row(r) if src is None else src
                self.sib_ids.append((r, send(src, self.row(r), sib)))

        def begin(self, src):
            self.ids = [send(src, self.row(0), self.at(1)), send(src, self.row(0), self.at(3))]
            self.pass_on(0, src)

        def middle(self):
            got(self.row(3), self.ids[0])
            self.ids.append(send(self.row(3, 0), self.row(3, 0), self.at(1)))
            self.pass_on(3)
            got(self.row(1), self.ids[1])
            self.ids.append(send(self.row(1, 1), self.row(1, 1), self.at(3)))
            self.pass_on(1)

        def end(self):
            got(self.row(2, 0), self.ids[2])
            got(self.row(2, 1), self.ids[3])
            self.pass_on(2)

        def close(self):
            for r, i in self.sib_ids:
                got(self.to_sib(r), i)

    def spot(ref, base, n, h=ALL):
        if h is ALL:
            return ref.at[pl.ds(al(base), n)]
        return ref.at[pl.ds(al(base + h * (n // 2)), n // 2)]

    def chunk_id(k):
        out = p * 0
        for i, (rel, h) in enumerate(ORDER):
            out = jnp.where(k == i, rem4(p + rel) * 2 + h, out)
        return out

    def is_dt(s):
        return (s >= 4) & (s < 12)

    def chunk_at(s):
        return jnp.where(is_dt(s), s - 4, chunk_id(jnp.where(s < 4, s, s - 8)))

    def loads(s):
        slot = lax.rem(s, 2)
        r = chunk_at(s) * CH
        return [pltpu.make_async_copy(e_hbm.at[pl.ds(al(r, 16), CH)], eb.at[slot], esem.at[slot])] + [
            pltpu.make_async_copy(z_hbm.at[n, pl.ds(al(r), CH)], zb.at[slot, n], zsem.at[slot, n]) for n in range(NT)]

    t_load = pltpu.make_async_copy(t_hbm, tb, lsem.at[0])
    h_load = pltpu.make_async_copy(h_hbm.at[pl.ds(al((core * 4 + x) * NR, 16), NR)], hown, lsem.at[1])
    for cp in loads(jnp.int32(0)):
        cp.start()
    t_load.start()
    h_load.start()

    barrier = pltpu.get_barrier_semaphore()
    peers = [f(r) for f in (at_y, at_z) for r in RING] + [at_t(r) for r in range(1, 8)]
    for dev in peers:
        pl.semaphore_signal(barrier, inc=1, device_id=dev, device_id_type=MESH)
    wsum = jnp.zeros((1, 1), F32)
    for n in range(NT):
        wsum = wsum + jnp.sum(meta[n, LIVE, :], **COLS)
    dnp[yc] = jnp.broadcast_to(wsum, dnp.shape[1:])
    srecv[tp] = meta[...]
    pl.semaphore_wait(barrier, len(peers))

    ids_y = share(dnp, yc, at_y)
    ids_t = [send(meta, srecv.at[tp], at_t(r)) for r in range(1, 8)]
    dt[...] = jnp.zeros_like(dt)
    for k in (0, 2, 4, 6, 12, 14):
        de[k:k + 2] = jnp.zeros((2, BLK, D), F32)
    vb[...] = jnp.zeros_like(vb)
    dnq[zc] = shared(dnp, yc, ids_y)
    ids_z = share(dnq, zc, at_z)
    for r, i in zip(range(1, 8), ids_t):
        got(srecv.at[rem8(tp - r)], i)
    tiles = []
    for n in range(NT):
        mx = srecv[0, n, MAX, :]
        for k in range(1, 8):
            mx = jnp.maximum(mx, srecv[k, n, MAX, :])
        tot = jnp.zeros((1, TT), F32)
        tgt = jnp.zeros((1, TT), F32)
        for k in range(8):
            tot = tot + srecv[k, n, SUM, :] * jnp.exp(srecv[k, n, MAX, :] - mx)
            tgt = tgt + srecv[k, n, TGT, :]
        lab = meta[n, LAB, :] - (tp * d.V).astype(F32)
        comb[n, LAB, :] = mx
        comb[n, LIVE, :] = 1.0 / tot
        comb[n, MAX, :] = jnp.where(lab < d.V, lab, -1.0)
        tiles.append(jnp.log(tot) + mx - tgt)
    denom = shared(dnq, zc, ids_z)[LAB, LAB] + LOSS_EPS
    ce = jnp.zeros((1, TT), F32)
    for n in range(NT):
        w = meta[n, LIVE, :]
        c = w / denom
        comb[n, LIVE, :] = comb[n, LIVE, :] * c
        comb[n, SRC, :] = c
        ce = ce + w * tiles[n]
    ce = jnp.sum(ce, **COLS) / denom
    t_load.wait()

    sub = lax.broadcasted_iota(I32, (16, TT), 0)
    row8 = lax.broadcasted_iota(I32, (NCH, LANES), 0)
    dacc[CH:, :] = jnp.zeros((d.CL - CH, LANES), F32)

    def grads(slot, n, cid, sums):
        m8 = jnp.broadcast_to(comb[n, LAB, :], (16, TT))
        a8 = jnp.broadcast_to(comb[n, LIVE, :], (16, TT))
        c8 = jnp.broadcast_to(comb[n, SRC, :], (16, TT))
        l8 = jnp.broadcast_to(comb[n, MAX, :].astype(I32) - cid * CH, (16, TT))
        live = c8 > 0
        for i in range(CH // 16):
            rows = slice(i * 16, (i + 1) * 16)
            g = jnp.exp(zb[slot, n, rows, :] - m8) * a8
            g = g - jnp.where(sub + i * 16 == l8, c8, 0.0)
            g = jnp.where(live, g, 0.0)
            dzb[n % 2, rows, :] = g.astype(BF16)
            if sums:
                part = sum(g[:, cols] for cols in cuts(TT))
                dacc[rows, :] = part if n == 0 else dacc[rows, :] + part

    two = [de.at[pl.ds(2 * k, 2)] for k in range(8)]
    lo, hi = pl.ds(0, 2), pl.ds(2, 2)
    stage1 = [link(two[0], two[4], at_p(1)), link(two[1], two[5], at_p(3)),
              link(two[2], fm.at[hi], at_p(1)), link(two[3], fp.at[lo], at_p(3)),
              link(two[4], fm.at[lo], at_p(1)), link(two[5], fp.at[hi], at_p(3))]
    to_sib = link(dt.at[pl.ds(al(other * HN), HN)], dr, sib)

    def add2(dst, src):
        for b in range(2):
            add(dst.at[b], [src.at[b]])

    def xrow(r, h=ALL):
        return spot(dt, (core * 4 + rem4(x + r)) * NR, NR, h)

    rs_x = Scatter(xrow, xa, xb, xm, xp, at_x)

    def step(s, carry):
        slot = lax.rem(s, 2)
        for cp in loads(s):
            cp.wait()

        @pl.when(s < 15)
        def _():
            for cp in loads(s + 1):
                cp.start()

        cid = chunk_at(s)

        @pl.when(is_dt(s))
        def _():
            for n in range(NT):
                grads(slot, n, cid, False)
                dt[n * TT:(n + 1) * TT, :] += mm(dzb[n % 2], eb[slot], TN)

        @pl.when(s == 11)
        def _():
            listed[to_sib].start()

        @pl.when(jnp.logical_not(is_dt(s)))
        def _():
            k = jnp.where(s < 4, s, s - 8)
            for i in (0, 1):
                @pl.when(k == i + 4)
                def _(i=i):
                    got(two[i + 4], stage1[i])
            for n in range(NT):
                grads(slot, n, cid, True)
                prod = mm(dzb[n % 2], tb[n * TT:(n + 1) * TT, :]).reshape(2, BLK, D)
                de[pl.ds(2 * k, 2)] += prod
            for cols in cuts(d.CL):
                tot = jnp.broadcast_to(jnp.sum(dacc[cols, :].T, **ROWS), (NCH, LANES))
                vb[:NCH, cols] = jnp.where(row8 == cid, tot, vb[:NCH, cols])
            for i in range(6):
                @pl.when(k == i)
                def _(i=i):
                    listed[stage1[i]].start()

        return carry

    lax.fori_loop(0, 16, step, 0)

    got(dr, to_sib)
    add(dt.at[pl.ds(al(core * HN), HN)], [dr])
    rs_x.begin()
    own = de.at[pl.ds(12, 4)]
    got(fp.at[lo], stage1[3])
    add2(own.at[lo], fp.at[lo])
    got(fm.at[hi], stage1[2])
    add2(own.at[hi], fm.at[hi])
    vb[NCH:, :] = jnp.broadcast_to(ce, (NCH, d.CL))
    vby[yc] = vb[...]
    ids_y = share(vby, yc, at_y)
    h_load.wait()
    ub[...] = mm(hown[...], wt_ref[...]) + row_of(bt_ref)
    gamma = row_of(gm_ref)
    rs_x.middle()

    got(fm.at[lo], stage1[4])
    add2(own.at[lo], fm.at[lo])
    got(fp.at[hi], stage1[5])
    add2(own.at[hi], fp.at[hi])

    def ob(r, h=ALL):
        blk = own.at[rem4(q + r)]
        return blk if h is ALL else half(blk, h)

    rs_q = Scatter(ob, r2a, r2b, f2m, f2p, at_q)
    rs_q.begin()
    vbz[zc] = shared(vby, yc, ids_y)
    ids_z = share(vbz, zc, at_z)
    rs_q.middle()
    rs_q.end()
    fin = ob(0)
    add(fin, [f2m, f2p])

    def orow(rp, rq, h=ALL):
        return spot(de_out, (rem4(p + rp) * 4 + rem4(q + rq)) * BLK, BLK, h)

    ag_q = Gather(lambda r, h=ALL: orow(0, r, h), at_q)
    ag_q.begin(fin)
    keep = [pltpu.make_async_copy(fin, orow(0, 0), osem.at[0])]
    keep[0].start()
    ag_p = [Gather(lambda r, h=ALL, j=j: orow(r, j, h), at_p) for j in FINISH]

    rs_x.end()
    lb = 64 if NR % 64 == 0 else 16
    dtown = xrow(0)
    vec[...] = jnp.zeros_like(vec)

    def back(i, carry):
        rows = pl.ds(al(i * lb, 16), lb)
        u = ub[rows, :]
        cdf = 0.5 * (1.0 + lax.erf(u * RSQRT2))
        a = u * cdf
        ctr = a - jnp.mean(a, **COLS)
        rstd = lax.rsqrt(jnp.mean(ctr * ctr, **COLS) + LN_EPS)
        xh = ctr * rstd
        g = dtown[rows, :] + xm[rows, :] + xp[rows, :]
        gx = g * xh
        gg = g * gamma
        m1 = jnp.mean(gg, **COLS)
        m2 = jnp.mean(gg * xh, **COLS)
        da = rstd * (gg - m1 - xh * m2)
        pdf = jnp.exp(u * u * -0.5) * 0.3989422804014327
        du = da * (cdf + u * pdf)
        dub[rows, :] = du.astype(BF16)
        for j, v in enumerate((gx, g, du)):
            vec[j] += jnp.sum(v.reshape(lb // GB, GB, D), axis=0)
        return carry

    lax.fori_loop(0, NR // lb, back, 0)
    listed[to_sib].wait_send()
    dwt = dt.at[pl.ds(al(other * HN), D)]
    for cols in cuts(D):
        dwt[:, cols] = mm(hown[...], dub[:, cols], TN)
    i_wr = send(dwt.at[pl.ds(al(other * HD), HD)], wr, sib)
    ag_p[0].begin(fin)
    vect[tp] = jnp.concatenate([jnp.sum(vec[i], **ROWS) for i in range(GB)], axis=0)
    ids_t = [send(vect.at[tp], vect.at[tp], at_t(r)) for r in range(1, 8)]
    for cols in cuts(D):
        ub[:, cols] = mm(dub[...], wt_ref[cols, :], NTR).astype(BF16).astype(F32)

    def wrow(r, h=ALL):
        return spot(dwt, core * HD + rem4(x + r) * WR, WR, h)

    rs_w = Scatter(wrow, wxa, wxb, wxm, wxp, at_x)
    got(wr, i_wr)
    add(dwt.at[pl.ds(al(core * HD), HD)], [wr])
    rs_w.begin()
    ag_q.middle()
    ag_p[1].begin(orow(0, 3))
    ag_p[2].begin(orow(0, 1))
    rs_w.middle()

    def hrow(c):
        return lambda r, h=ALL: spot(dh_out, (c * 4 + rem4(x + r)) * NR, NR, h)

    ag_h = Gather(hrow(core), at_x, hrow(other))
    ag_h.begin(ub)
    keep.append(pltpu.make_async_copy(ub, hrow(core)(0), osem.at[1]))
    keep[1].start()

    for r, i in zip(range(1, 8), ids_t):
        got(vect.at[rem8(tp - r)], i)
    acc = vect[0]
    for k in range(1, 8):
        acc = acc + vect[k]
    vecy[yc] = acc
    ids_y = share(vecy, yc, at_y)

    rs_w.end()
    wown = wrow(0)
    add(wown, [wxm, wxp])

    def piece(ref, k):
        return ref.at[pl.ds(al(k * WP), WP)]

    ids_q = [send(piece(wown, rem4(q + r)), wq.at[q], at_q(r)) for r in RING]
    wq[q] = piece(wown, q)[...]
    ag_q.end()
    ag_p[3].begin(orow(0, 2))
    wp[p] = shared(wq, q, ids_q)
    ids_p = share(wp, p, at_p)
    ag_p[0].middle()
    dbo_out[...] = shared(vbz, zc, ids_z)
    vecz[zc] = shared(vecy, yc, ids_y)
    ids_z = share(vecz, zc, at_z)
    piece(wag, q)[...] = shared(wp, p, ids_p)
    ids_q = [send(piece(wag, q), piece(wag, q), at_q(r)) for r in RING]
    ag_p[1].middle()
    for r, i in zip(RING, ids_q):
        got(piece(wag, rem4(q - r)), i)

    def grow(c):
        return lambda r, h=ALL: spot(dwt_out, c * HD + rem4(x + r) * WR, WR, h)

    ag_w = Gather(grow(core), at_x, grow(other))
    ag_w.begin(wag)
    keep.append(pltpu.make_async_copy(wag, grow(core)(0), osem.at[2]))
    keep[2].start()
    ag_h.middle()
    ag_p[2].middle()
    vec_out[...] = shared(vecz, zc, ids_z)
    ag_h.end()
    ag_w.middle()
    ag_p[3].middle()
    ag_w.end()

    ag_h.close()
    ag_w.close()
    for g in ag_p:
        g.end()
    for cp in keep:
        cp.wait()
    for i, cp in enumerate(listed):
        if i != to_sib:
            cp.wait_send()


def train(d, t, h, z, meta, e, w_t, bt, gm, be):
    any_ = pl.BlockSpec(memory_space=pl.ANY)
    vm = pl.BlockSpec(memory_space=pltpu.VMEM)
    sd = jax.ShapeDtypeStruct
    D, BLK, CH, TT, NR, WR = d.D, d.BLK, d.CH, d.TT, d.NR, d.WR

    def vf(*shape):
        return pltpu.VMEM((*shape, D), F32)

    def vl(*shape):
        return pltpu.VMEM(shape, F32)

    def vh(*shape):
        return pltpu.VMEM(shape, BF16)

    def twice(v):
        return [v, v]

    dma = pltpu.SemaphoreType.DMA
    return pl.pallas_call(
        functools.partial(train_kernel, d),
        out_shape=(sd((d.VP, D), F32), sd((d.N, D), F32), sd((D, D), F32), sd((GB, D), F32), sd((2 * NCH, d.CL), F32)),
        in_specs=[any_, any_, any_, vm, any_, vm, vm, vm, vm],
        out_specs=(any_, any_, any_, vm, vm),
        scratch_shapes=[
            vh(d.N, D), vh(2, CH, D), vl(2, NT, CH, TT), vh(2, CH, TT), vf(d.N), vf(16, BLK), *twice(vf(4, BLK)),
            *twice(vf(d.HB)), *twice(vf(BLK)), vf(d.HN), *twice(vf(d.HR)), *twice(vf(NR)),
            vf(NR), *twice(vh(NR, D)), vf(d.HD), *twice(vf(WR // 2)), *twice(vf(WR)), *twice(vf(4, d.WP)), vf(WR),
            vl(8, NT, 8, TT), vl(NT, 8, TT), vl(d.CL, LANES), vl(2 * NCH, d.CL), *twice(vl(4, 2 * NCH, d.CL)),
            *twice(vl(4, GB, LANES)), *twice(vf(GB, GB)), *twice(vf(4, GB)),
            dma((2,)), dma((2,)), dma((2, NT)), dma((3,)), *twice(dma((NSEM,))),
        ],
        compiler_params=pltpu.CompilerParams(vmem_limit_bytes=VMEM_MAX, collective_id=0, has_side_effects=True),
        name="mlm_train",
    )(t, h, z, meta, e, w_t, bt, gm, be)


def finish_kernel(d, cnt_hbm, col_hbm, dh_hbm, de_hbm, dwt_hbm, vec_ref, dbo_ref,
                  dH, dE, dW, g_out, b_out, t_out, loss,
                  cnt, colb, dhb, stage, wstage, outb, isem, csem, osem, dsem, esem, ssem):
    rows_g = GB * d.L
    src_iota = lax.broadcasted_iota(I32, (d.S, rows_g), 1)
    r_iota = lax.broadcasted_iota(I32, (d.S, 1), 0)
    first = pltpu.make_async_copy(cnt_hbm, cnt, ssem.at[0])
    first.start()
    parts = [(c * d.CH, min(d.CH, d.V - c * d.CH)) for c in range(NCH)]
    ins = [pltpu.make_async_copy(de_hbm.at[pl.ds(r, n)], stage.at[pl.ds(r, n)], dsem.at[i])
           for i, (r, n) in enumerate(parts)]
    outs = [pltpu.make_async_copy(stage.at[pl.ds(r, n)], dE.at[pl.ds(r, n)], esem.at[i])
            for i, (r, n) in enumerate(parts)]
    ins.append(pltpu.make_async_copy(dwt_hbm, wstage, dsem.at[NCH]))
    outs.append(pltpu.make_async_copy(wstage, dW, esem.at[NCH]))

    def loads(o, slot):
        o = pl.multiple_of(o, 16)
        return [pltpu.make_async_copy(dh_hbm.at[pl.ds(o, d.S)], dhb.at[slot], isem.at[slot]),
                pltpu.make_async_copy(col_hbm.at[pl.ds(o, d.S)], colb.at[slot], csem.at[slot])]

    def out_copy(g, slot):
        return pltpu.make_async_copy(outb.at[slot], dH.at[pl.ds(g * rows_g, rows_g)], osem.at[slot])

    for cp in loads(jnp.int32(0), 0):
        cp.start()
    for cp in ins:
        cp.start()
    for row, ref in ((LAB, g_out), (LIVE, b_out), (SRC, t_out)):
        for i, cols in enumerate(cuts(d.D)):
            ref[slice(i, i + 1), :] = vec_ref[row, cols]
    loss[...] = dbo_ref[NCH:NCH + 1, LAB]
    first.wait()

    def group(g, o):
        slot = lax.rem(g, 2)
        oslot = lax.rem(g, NBUF)
        c = cnt[0, g * GB]
        for j in range(1, GB):
            c = c + cnt[0, g * GB + j]
        nxt = o + ((c + 15) // 16) * 16

        @pl.when(g + 1 < d.G)
        def _():
            for cp in loads(nxt, 1 - slot):
                cp.start()

        for cp in loads(o, slot):
            cp.wait()

        @pl.when(g >= NBUF)
        def _():
            out_copy(g - NBUF, oslot).wait()

        src = jnp.where(r_iota < c, colb[slot, :, SRC].astype(I32), -1)
        hot = (src_iota == src).astype(BF16)
        outb[oslot] = mm(hot, dhb[slot].astype(BF16), TN).astype(BF16)
        out_copy(g, oslot).start()

        for i, (a, b) in enumerate(zip(ins, outs)):
            @pl.when(g == min(i, d.G - 1))
            def _(a=a, b=b):
                a.wait()
                b.start()

        return nxt

    lax.fori_loop(0, d.G, group, jnp.int32(0))
    for g in range(d.G - NBUF, d.G):
        out_copy(g, g % NBUF).wait()
    for cp in outs:
        cp.wait()


def finish(d, cnt, col, dh, de, dwt, vec, dbo):
    any_ = pl.BlockSpec(memory_space=pl.ANY)
    vm = pl.BlockSpec(memory_space=pltpu.VMEM)
    sd = jax.ShapeDtypeStruct
    dma = pltpu.SemaphoreType.DMA
    row = sd((d.D // LANES, LANES), F32)
    return pl.pallas_call(
        functools.partial(finish_kernel, d),
        out_shape=(sd((d.B * d.L, d.D), BF16), sd((d.V, d.D), F32), sd((d.D, d.D), F32), row, row, row, sd((1, 1), F32)),
        in_specs=[any_, any_, any_, any_, any_, vm, vm],
        out_specs=(any_, any_, any_, vm, vm, vm, vm),
        scratch_shapes=[
            pltpu.SMEM((GB, d.B), I32), pltpu.VMEM((2, d.S, LANES), F32), pltpu.VMEM((2, d.S, d.D), F32),
            pltpu.VMEM((d.VP, d.D), F32), pltpu.VMEM((d.D, d.D), F32), pltpu.VMEM((NBUF, GB * d.L, d.D), BF16),
            dma((2,)), dma((2,)), dma((NBUF,)), dma((NCH + 1,)), dma((NCH + 1,)), dma((1,)),
        ],
        compiler_params=pltpu.CompilerParams(vmem_limit_bytes=VMEM_MAX),
        name="mlm_finish",
    )(cnt, col, dh, de, dwt, vec, dbo)


def solution(mesh):
    def step(hidden, positions, labels, weights, w_t, b_t, gamma, beta, embed, out_bias):
        d = Dims(hidden.shape, positions.shape, embed.shape)
        bias = jnp.pad(out_bias, (0, d.VP - d.V), constant_values=PAD_BIAS).reshape(-1, LANES)
        bt, gm, be = (v.reshape(-1, LANES) for v in (b_t, gamma, beta))
        h, t, z, meta, col, e, cnt = forward(d, hidden.reshape(-1, d.D), positions.T, labels.T, weights.T,
                                             w_t, bt, gm, be, embed, bias)
        de, dh, dwt, vec, dbo = train(d, t, h, z, meta, e, w_t, bt, gm, be)
        d_hidden, d_embed, d_w, d_gamma, d_beta, d_bt, loss = finish(d, cnt, col, dh, de, dwt, vec, dbo)
        d_bias = dbo[:NCH, :d.CH].reshape(-1)[:d.V]
        return (loss.reshape(()), d_hidden.reshape(hidden.shape), d_w, d_bt.reshape(-1), d_gamma.reshape(-1),
                d_beta.reshape(-1), d_embed, d_bias)

    rows, vocab, whole = P("dp"), P("tp"), P()
    return jax.shard_map(step, mesh=mesh, check_vma=False,
                         in_specs=(rows, rows, rows, rows, whole, whole, whole, whole, vocab, vocab),
                         out_specs=(whole, rows, whole, whole, whole, whole, vocab, vocab))
```

time: 590 us -> 260 us (0.44); the launches traced: 582 us -> 258 us
  Pallas kernels: 0 us -> 255 us
  blocking collectives: 172 us -> 0 us
  waiting for transfers between devices: 148 us -> 0 us
  matrix products: 140 us -> 0 us
  other arithmetic: 74.2 us -> 0 us
  local copies, waits for them, and re-layouts: 29.9 us -> 2.73 us
  between operations: 16.8 us -> 0.81 us
    pallas_call x0 -> x3, Pallas kernels: none -> 255 us  [the longest x1 187 us: train(): pl.pallas_call(functools.partial(train_kernel, d), out_shape=(sd((d.VP, D...]
    psum x2 -> x0, waiting for transfers between devices: 148 us -> none  [the longest x1 77.1 us: local_step(): lax.psum(jnp.einsum('nd,ne->de', tok_rows, d_pre_bf, preferred_element_ty...]
    psum x4 -> x0, blocking collectives: 144 us -> none  [the longest x1 62.8 us: local_step(): loss = lax.psum(jnp.sum(flat_w * (log_norm - target_logit)), 'dp') / denom]
    dot_general x8 -> x0, matrix products: 140 us -> none  [the longest x1 25 us: local_step(): jnp.einsum('nd,vd->nv', t_bf, embed, preferred_element_type=jnp.float32)]
    reduce_sum x8 -> x0, other arithmetic: 73.4 us -> none  [the longest x1 30.1 us: local_step(): d_out_bias = lax.psum(jnp.sum(d_logits, axis=0), 'dp')]
    pmax x1 -> x0, blocking collectives: 27.9 us -> none  [local_step(): row_max = lax.pmax(jnp.max(logits, axis=1), 'tp')]
    unnamed x32 -> x0, local copies, waits for them, and re-layouts: 15.8 us -> none
    reshape x3 -> x2, local copies, waits for them, and re-layouts: 13.9 us -> 2.01 us  [the longest x1 1.33 us: step(): jnp.pad(out_bias, (0, d.VP - d.V), constant_values=PAD_BIAS)]
  transfers between devices with their start and end apart: 2 -> 0, of which waited for: 2 -> 0; matrix products, arithmetic and copies ran while one was open for 10% -> 0% of each run, Pallas kernels for 0% -> 0%
where the time goes in v1:
time: 260 us; the launch traced here: 258 us
  Pallas kernels  255 us (98%)
  local copies, waits for them, and re-layouts  2.73 us (1%)
    pallas_call x1, Pallas kernels, train(): pl.pallas_call(functools.partial(train_kernel, d), out_shape=(sd((d.VP, D...  187 us
    pallas_call x1, Pallas kernels, forward(): pl.pallas_call(functools.partial(forward_kernel, d), out_shape=(sd((d.N,...  42.6 us
    pallas_call x1, Pallas kernels, finish(): pl.pallas_call(functools.partial(finish_kernel, d), out_shape=(sd((d.B *...  25.3 us

profile of v1, /device:TPU:1, one launch (start us, length us, event | category | flops | bytes accessed | tf_op | source)
XLA Modules:
  0.0 258.2 jit_solution(5617911551368761021)
XLA Ops:
  0.6 1.3 pad_bitcast_fusion.bias_ref
  2.0 42.6 %mlm_forward.1 = (bf16[2560,768]{1,0:T(8,128)(2,1)}, bf16[2560,768]{1,0:T(8,128)(2,1)}, f32[5,3840,512]{2,1,0:T(8,128)}, f32[5,8,512]{2,1,0:T(8,128)}, f32[2560,...) custom-call(bf16[16384,768]{1,0:T(8,128)(2,1)} %bitcast.15, s32[20,128]{1,0:T(8,128)} %bitcast.23, ...), custom_call_target="tpu_custom_call" | custom-call | tf_op jit(solution)/shard_map/mlm_forward/pallas_call | solution.py:230
  44.6 186.7 %mlm_train.1 = (f32[3840,768]{1,0:T(8,128)}, f32[2560,768]{1,0:T(8,128)}, f32[768,768]{1,0:T(8,128)}, f32[8,768]{1,0:T(8,128)}, f32[16,512]{1,0:T(8,128)}) custom-call(bf16[2560,768]{1,0:T(8,128)(2,1)} %get-tuple-element.29.t_hbm, bf16[2560,768]{1,0:T(8,128)(2,1)} %get-tuple-element.30.h_hbm, f32[5,3840,512]{2,1,0:T(8,128)} %get-tuple-element.31.z_hbm, ...), custom_call_target="tpu_custom_call" | custom-call | tf_op jit(solution)/shard_map/mlm_train/pallas_call | solution.py:742
  231.3 0.7 slice.6
  232.0 0.7 reshape.59
  232.7 25.3 %mlm_finish.1 = (bf16[16384,768]{1,0:T(8,128)(2,1)}, f32[3824,768]{1,0:T(8,128)}, f32[768,768]{1,0:T(8,128)}, f32[6,128]{1,0:T(8,128)}, f32[6,128]{1,0:T(8,128)}, /*index=5*/f32[6,128]{1,0:T(8,128)}, f32[1,1]{1,0:T(1,128)}) custom-call(s32[8,128]{1,0:T(8,128)} %get-tuple-element.27.cnt_hbm, f32[2560,128]{1,0:T(8,128)} %get-tuple-element.28.col_hbm, ...), custom_call_target="tpu_custom_call" | custom-call | tf_op jit(solution)/shard_map/mlm_finish/pallas_call | solution.py:840

commit v2 on v1

--- a/solution.py
+++ b/solution.py
@@ -50,7 +50,7 @@
         self.HN, self.HD, self.HB, self.HR = self.N // 2, self.D // 2, self.BLK // 2, self.NR // 2
         self.WR = self.D // 8
         self.WP = self.WR // 4
-        self.CL = -(-self.CH // LANES) * LANES
+        self.CL = -(-self.BLK // LANES) * LANES
 
 
 def cuts(n):
@@ -257,15 +257,17 @@
 MESH = pl.DeviceIdType.MESH
 RING = (1, 2, 3)
 NSEM = 128
-ORDER = ((2, 0), (2, 1), (1, 1), (3, 0), (1, 0), (3, 1), (0, 0), (0, 1))
-FINISH = (0, 3, 1, 2)
+NEAR = (2, 1, 3, 0)
+CODES = "200210201211110300111301100310101311000010001011"
+ORDER = [tuple(int(c) for c in CODES[i:i + 3]) for i in range(0, len(CODES), 3)]
+STEPS = "pxxxpxxpppbpbxwvpp00wwvvwpvvww11ww22hhw033h1hww23ww"
 
 
 def train_kernel(d, t_hbm, h_hbm, z_hbm, meta, e_hbm, wt_ref, bt_ref, gm_ref, be_ref,
                  de_out, dh_out, dwt_out, vec_out, dbo_out,
                  tb, eb, zb, dzb, dt, de, fm, fp, r2a, r2b, f2m, f2p, dr, xa, xb, xm, xp,
-                 ub, dub, hown, wr, wxa, wxb, wxm, wxp, wp, wq, wag, srecv, comb, dacc, vb, vby, vbz,
-                 dnp, dnq, vec, vect, vecy, vecz, lsem, esem, zsem, osem, ss, rs):
+                 ub, dub, hown, wr, wxa, wxb, wxm, wxp, wq, wp, w1, w2, w3, w4, wag, srecv, comb, dacc, vb, vby, vbz,
+                 dnp, dnq, vec, vect, vecp, vecq, v1, v2, v3, v4, lsem, esem, zsem, osem, ss, rs):
     dp = lax.axis_index("dp")
     tp = lax.axis_index("tp")
     zc, yc = dp // 4, lax.rem(dp, 4)
@@ -274,7 +276,7 @@
     pm, qm = 1 + 3 * core, 4 - 3 * core
     p = yc + core * (zc - yc)
     q = zc + core * (yc - zc)
-    N, D, CH, BLK, TT, NR = d.N, d.D, d.CH, d.BLK, d.TT, d.NR
+    D, BLK, TT, NR = d.D, d.BLK, d.TT, d.NR
     HN, HD, WR, WP = d.HN, d.HD, d.WR, d.WP
 
     def rem4(v):
@@ -349,83 +351,25 @@
 
         lax.fori_loop(0, nr // step, body, 0)
 
-    class Scatter:
-        def __init__(self, blk, a, b, m, pp, at):
-            self.blk, self.a, self.b, self.m, self.pp, self.at = blk, a, b, m, pp, at
-
-        def begin(self):
-            blk, at = self.blk, self.at
-            self.ids = [send(blk(2, 0), self.a, at(1)), send(blk(2, 1), self.b, at(3)),
-                        send(blk(1, 1), half(self.m, 1), at(1)), send(blk(3, 0), half(self.pp, 0), at(3))]
-
-        def middle(self):
-            blk, at = self.blk, self.at
-            got(self.a, self.ids[0])
-            add(blk(1, 0), [self.a])
-            self.ids.append(send(blk(1, 0), half(self.m, 0), at(1)))
-            got(self.b, self.ids[1])
-            add(blk(3, 1), [self.b])
-            self.ids.append(send(blk(3, 1), half(self.pp, 1), at(3)))
-
-        def end(self):
-            ids = self.ids
-            got(half(self.m, 1), ids[2])
-            got(half(self.pp, 0), ids[3])
-            got(half(self.m, 0), ids[4])
-            got(half(self.pp, 1), ids[5])
-
-    class Gather:
-        def __init__(self, row, at, to_sib=None):
-            self.row, self.at, self.to_sib, self.sib_ids = row, at, to_sib, []
-
-        def pass_on(self, r, src=None):
-            if self.to_sib is not None:
-                src = self.row(r) if src is None else src
-                self.sib_ids.append((r, send(src, self.row(r), sib)))
-
-        def begin(self, src):
-            self.ids = [send(src, self.row(0), self.at(1)), send(src, self.row(0), self.at(3))]
-            self.pass_on(0, src)
-
-        def middle(self):
-            got(self.row(3), self.ids[0])
-            self.ids.append(send(self.row(3, 0), self.row(3, 0), self.at(1)))
-            self.pass_on(3)
-            got(self.row(1), self.ids[1])
-            self.ids.append(send(self.row(1, 1), self.row(1, 1), self.at(3)))
-            self.pass_on(1)
-
-        def end(self):
-            got(self.row(2, 0), self.ids[2])
-            got(self.row(2, 1), self.ids[3])
-            self.pass_on(2)
-
-        def close(self):
-            for r, i in self.sib_ids:
-                got(self.to_sib(r), i)
-
     def spot(ref, base, n, h=ALL):
         if h is ALL:
             return ref.at[pl.ds(al(base), n)]
         return ref.at[pl.ds(al(base + h * (n // 2)), n // 2)]
 
-    def chunk_id(k):
+    first_of = (jnp.where((q == 1) | (q == 2), 0, 1), jnp.where((q == 1) | (q == 2), 3, 2))
+
+    def block_id(k):
         out = p * 0
-        for i, (rel, h) in enumerate(ORDER):
-            out = jnp.where(k == i, rem4(p + rel) * 2 + h, out)
+        for i, (rel, h, second) in enumerate(ORDER):
+            b = 4 * h + 1 - first_of[h] if second else first_of[h]
+            out = jnp.where(k == i, rem4(p + rel) * 4 + b, out)
         return out
 
-    def is_dt(s):
-        return (s >= 4) & (s < 12)
-
-    def chunk_at(s):
-        return jnp.where(is_dt(s), s - 4, chunk_id(jnp.where(s < 4, s, s - 8)))
-
-    def loads(s):
-        slot = lax.rem(s, 2)
-        r = chunk_at(s) * CH
-        return [pltpu.make_async_copy(e_hbm.at[pl.ds(al(r, 16), CH)], eb.at[slot], esem.at[slot])] + [
-            pltpu.make_async_copy(z_hbm.at[n, pl.ds(al(r), CH)], zb.at[slot, n], zsem.at[slot, n]) for n in range(NT)]
+    def loads(k):
+        slot = lax.rem(k, 2)
+        r = block_id(k) * BLK
+        return [pltpu.make_async_copy(e_hbm.at[pl.ds(al(r, 16), BLK)], eb.at[slot], esem.at[slot])] + [
+            pltpu.make_async_copy(z_hbm.at[n, pl.ds(al(r), BLK)], zb.at[slot, n], zsem.at[slot, n]) for n in range(NT)]
 
     t_load = pltpu.make_async_copy(t_hbm, tb, lsem.at[0])
     h_load = pltpu.make_async_copy(h_hbm.at[pl.ds(al((core * 4 + x) * NR, 16), NR)], hown, lsem.at[1])
@@ -448,8 +392,8 @@
     ids_y = share(dnp, yc, at_y)
     ids_t = [send(meta, srecv.at[tp], at_t(r)) for r in range(1, 8)]
     dt[...] = jnp.zeros_like(dt)
-    for k in (0, 2, 4, 6, 12, 14):
-        de[k:k + 2] = jnp.zeros((2, BLK, D), F32)
+    for k in (*range(8), *range(12, 16)):
+        de[k] = jnp.zeros((BLK, D), F32)
     vb[...] = jnp.zeros_like(vb)
     dnq[zc] = shared(dnp, yc, ids_y)
     ids_z = share(dnq, zc, at_z)
@@ -482,241 +426,324 @@
     t_load.wait()
 
     sub = lax.broadcasted_iota(I32, (16, TT), 0)
-    row8 = lax.broadcasted_iota(I32, (NCH, LANES), 0)
-    dacc[CH:, :] = jnp.zeros((d.CL - CH, LANES), F32)
-
-    def grads(slot, n, cid, sums):
+    row16 = lax.broadcasted_iota(I32, (16, LANES), 0)
+    dacc[BLK:, :] = jnp.zeros((d.CL - BLK, LANES), F32)
+
+    def grads(slot, n, cid):
         m8 = jnp.broadcast_to(comb[n, LAB, :], (16, TT))
         a8 = jnp.broadcast_to(comb[n, LIVE, :], (16, TT))
         c8 = jnp.broadcast_to(comb[n, SRC, :], (16, TT))
-        l8 = jnp.broadcast_to(comb[n, MAX, :].astype(I32) - cid * CH, (16, TT))
+        l8 = jnp.broadcast_to(comb[n, MAX, :].astype(I32) - cid * BLK, (16, TT))
         live = c8 > 0
-        for i in range(CH // 16):
+        for i in range(BLK // 16):
             rows = slice(i * 16, (i + 1) * 16)
             g = jnp.exp(zb[slot, n, rows, :] - m8) * a8
             g = g - jnp.where(sub + i * 16 == l8, c8, 0.0)
             g = jnp.where(live, g, 0.0)
             dzb[n % 2, rows, :] = g.astype(BF16)
-            if sums:
-                part = sum(g[:, cols] for cols in cuts(TT))
-                dacc[rows, :] = part if n == 0 else dacc[rows, :] + part
-
-    two = [de.at[pl.ds(2 * k, 2)] for k in range(8)]
-    lo, hi = pl.ds(0, 2), pl.ds(2, 2)
-    stage1 = [link(two[0], two[4], at_p(1)), link(two[1], two[5], at_p(3)),
-              link(two[2], fm.at[hi], at_p(1)), link(two[3], fp.at[lo], at_p(3)),
-              link(two[4], fm.at[lo], at_p(1)), link(two[5], fp.at[hi], at_p(3))]
-    to_sib = link(dt.at[pl.ds(al(other * HN), HN)], dr, sib)
-
-    def add2(dst, src):
-        for b in range(2):
-            add(dst.at[b], [src.at[b]])
+            part = sum(g[:, cols] for cols in cuts(TT))
+            dacc[rows, :] = part if n == 0 else dacc[rows, :] + part
+
+    stage1 = [link(de.at[k], de.at[k + 8], at_p(3 if k % 2 else 1)) for k in range(4)]
+    stage1 += [link(de.at[k], (fp if k % 2 else fm).at[(k - 4) // 2], at_p(3 if k % 2 else 1)) for k in range(4, 12)]
+    to_sib = [link(dt.at[pl.ds(al((other * 4 + rem4(x + r)) * NR), NR)], dr.at[rem4(x + r)], sib) for r in NEAR]
+
+    def step(k, carry):
+        slot = lax.rem(k, 2)
+        for cp in loads(k):
+            cp.wait()
+
+        @pl.when(k < 15)
+        def _():
+            for cp in loads(k + 1):
+                cp.start()
+
+        for i in range(4):
+            @pl.when(k == i + 8)
+            def _(i=i):
+                got(de.at[i + 8], stage1[i])
+        cid = block_id(k)
+        for n in range(NT):
+            grads(slot, n, cid)
+            de[k] += mm(dzb[n % 2], tb[n * TT:(n + 1) * TT, :])
+            dt[n * TT:(n + 1) * TT, :] += mm(dzb[n % 2], eb[slot], TN)
+        for cols in cuts(d.CL):
+            tot = jnp.broadcast_to(jnp.sum(dacc[cols, :].T, **ROWS), (16, LANES))
+            vb[:16, cols] = jnp.where(row16 == cid, tot, vb[:16, cols])
+        for i in range(12):
+            @pl.when(k == i)
+            def _(i=i):
+                listed[stage1[i]].start()
+
+        return carry
+
+    lax.fori_loop(0, 16, step, 0)
+    for i in to_sib:
+        listed[i].start()
+    vb[16:, :] = jnp.broadcast_to(ce, (GB, d.CL))
+    vby[yc] = vb[...]
+    ids_vy = share(vby, yc, at_y)
+
+    flows = {}
+    keep = []
+
+    def copy_out(src, dst):
+        keep.append(pltpu.make_async_copy(src, dst, osem.at[len(keep)]))
+        keep[-1].start()
+
+    def flow_b():
+        yield
+        vbz[zc] = shared(vby, yc, ids_vy)
+        ids = share(vbz, zc, at_z)
+        yield
+        dbo_out[...] = shared(vbz, zc, ids)
+
+    def orow(rp, rq, h=ALL):
+        return spot(de_out, (rem4(p + rp) * 4 + rem4(q + rq)) * BLK, BLK, h)
+
+    def own(r, h=ALL):
+        b = rem4(q + r)
+        side = b // 2
+        head = first_of[0] + side * (first_of[1] - first_of[0])
+        blk = de.at[12 + side + jnp.where(b == head, 0, 2)]
+        return blk if h is ALL else half(blk, h)
+
+    def scatter_rest(blk, a, b, m, pp, at, ids):
+        yield
+        got(a, ids[0])
+        add(blk(1, 0), [a])
+        ids.append(send(blk(1, 0), half(m, 0), at(1)))
+        yield
+        got(b, ids[1])
+        add(blk(3, 1), [b])
+        ids.append(send(blk(3, 1), half(pp, 1), at(3)))
+
+    def scatter_end(m, pp, ids):
+        got(half(m, 1), ids[2])
+        got(half(pp, 0), ids[3])
+        got(half(m, 0), ids[4])
+        got(half(pp, 1), ids[5])
+
+    def far(blk, a, b, at):
+        return [send(blk(2, 0), a, at(1)), send(blk(2, 1), b, at(3))]
+
+    def near(blk, m, pp, at):
+        return [send(blk(1, 1), half(m, 1), at(1)), send(blk(3, 0), half(pp, 0), at(3))]
+
+    def both(src, dst, at):
+        return [send(src, dst, at(1)), send(src, dst, at(3))]
+
+    def relay(j):
+        ids = both(orow(0, j) if j else own(0), orow(0, j), at_p)
+        for r, h in ((3, 0), (1, 1)):
+            yield
+            got(orow(r, j), ids[h])
+            ids.append(send(orow(r, j, h), orow(r, j, h), at_p(1 + 2 * h)))
+        yield
+        for h in (0, 1):
+            got(orow(2, j, h), ids[2 + h])
+
+    def begin(name, gen):
+        flows[name] = gen
+        return next(gen)
+
+    def flow_p():
+        yield
+        for k, i in ((4, 13), (5, 12), (6, 15), (7, 14)):
+            buf = (fp if k % 2 else fm).at[(k - 4) // 2]
+            got(buf, stage1[k])
+            add(de.at[i], [buf])
+        yield
+        for k in (8, 9):
+            buf = (fp if k % 2 else fm).at[2]
+            got(buf, stage1[k])
+            add(de.at[k + 4], [buf])
+        ids = far(own, r2a, r2b, at_q)
+        yield
+        for k in (10, 11):
+            buf = (fp if k % 2 else fm).at[3]
+            got(buf, stage1[k])
+            add(de.at[k + 4], [buf])
+        ids += near(own, f2m, f2p, at_q)
+        yield from scatter_rest(own, r2a, r2b, f2m, f2p, at_q, ids)
+        yield
+        scatter_end(f2m, f2p, ids)
+        fin = own(0)
+        add(fin, [f2m, f2p])
+        ids = both(fin, orow(0, 0), at_q)
+        copy_out(fin, orow(0, 0))
+        begin("0", relay(0))
+        for r, h in ((3, 0), (1, 1)):
+            yield
+            got(orow(0, r), ids[h])
+            ids.append(send(orow(0, r, h), orow(0, r, h), at_q(1 + 2 * h)))
+            begin("12"[h], relay(r))
+        yield
+        for h in (0, 1):
+            got(orow(0, 2, h), ids[2 + h])
+        begin("3", relay(2))
 
     def xrow(r, h=ALL):
         return spot(dt, (core * 4 + rem4(x + r)) * NR, NR, h)
 
-    rs_x = Scatter(xrow, xa, xb, xm, xp, at_x)
-
-    def step(s, carry):
-        slot = lax.rem(s, 2)
-        for cp in loads(s):
-            cp.wait()
-
-        @pl.when(s < 15)
-        def _():
-            for cp in loads(s + 1):
-                cp.start()
-
-        cid = chunk_at(s)
-
-        @pl.when(is_dt(s))
-        def _():
-            for n in range(NT):
-                grads(slot, n, cid, False)
-                dt[n * TT:(n + 1) * TT, :] += mm(dzb[n % 2], eb[slot], TN)
-
-        @pl.when(s == 11)
-        def _():
-            listed[to_sib].start()
-
-        @pl.when(jnp.logical_not(is_dt(s)))
-        def _():
-            k = jnp.where(s < 4, s, s - 8)
-            for i in (0, 1):
-                @pl.when(k == i + 4)
-                def _(i=i):
-                    got(two[i + 4], stage1[i])
-            for n in range(NT):
-                grads(slot, n, cid, True)
-                prod = mm(dzb[n % 2], tb[n * TT:(n + 1) * TT, :]).reshape(2, BLK, D)
-                de[pl.ds(2 * k, 2)] += prod
-            for cols in cuts(d.CL):
-                tot = jnp.broadcast_to(jnp.sum(dacc[cols, :].T, **ROWS), (NCH, LANES))
-                vb[:NCH, cols] = jnp.where(row8 == cid, tot, vb[:NCH, cols])
-            for i in range(6):
-                @pl.when(k == i)
-                def _(i=i):
-                    listed[stage1[i]].start()
-
-        return carry
-
-    lax.fori_loop(0, 16, step, 0)
-
-    got(dr, to_sib)
-    add(dt.at[pl.ds(al(core * HN), HN)], [dr])
-    rs_x.begin()
-    own = de.at[pl.ds(12, 4)]
-    got(fp.at[lo], stage1[3])
-    add2(own.at[lo], fp.at[lo])
-    got(fm.at[hi], stage1[2])
-    add2(own.at[hi], fm.at[hi])
-    vb[NCH:, :] = jnp.broadcast_to(ce, (NCH, d.CL))
-    vby[yc] = vb[...]
-    ids_y = share(vby, yc, at_y)
-    h_load.wait()
-    ub[...] = mm(hown[...], wt_ref[...]) + row_of(bt_ref)
-    gamma = row_of(gm_ref)
-    rs_x.middle()
-
-    got(fm.at[lo], stage1[4])
-    add2(own.at[lo], fm.at[lo])
-    got(fp.at[hi], stage1[5])
-    add2(own.at[hi], fp.at[hi])
-
-    def ob(r, h=ALL):
-        blk = own.at[rem4(q + r)]
-        return blk if h is ALL else half(blk, h)
-
-    rs_q = Scatter(ob, r2a, r2b, f2m, f2p, at_q)
-    rs_q.begin()
-    vbz[zc] = shared(vby, yc, ids_y)
-    ids_z = share(vbz, zc, at_z)
-    rs_q.middle()
-    rs_q.end()
-    fin = ob(0)
-    add(fin, [f2m, f2p])
-
-    def orow(rp, rq, h=ALL):
-        return spot(de_out, (rem4(p + rp) * 4 + rem4(q + rq)) * BLK, BLK, h)
-
-    ag_q = Gather(lambda r, h=ALL: orow(0, r, h), at_q)
-    ag_q.begin(fin)
-    keep = [pltpu.make_async_copy(fin, orow(0, 0), osem.at[0])]
-    keep[0].start()
-    ag_p = [Gather(lambda r, h=ALL, j=j: orow(r, j, h), at_p) for j in FINISH]
-
-    rs_x.end()
+    def rows_out(out, n):
+        def at(c):
+            return lambda r, h=ALL: spot(out, (c * 4 + rem4(x + r)) * n, n, h)
+
+        return at(core), at(other)
+
+    def gather_x(src, out, n):
+        mine, its = rows_out(out, n)
+        ids = both(src, mine(0), at_x)
+        sibs = [send(src, mine(0), sib)]
+        copy_out(src, mine(0))
+        for r, h in ((3, 0), (1, 1)):
+            yield
+            got(mine(r), ids[h])
+            ids.append(send(mine(r, h), mine(r, h), at_x(1 + 2 * h)))
+            sibs.append(send(mine(r), mine(r), sib))
+        yield
+        for h in (0, 1):
+            got(mine(2, h), ids[2 + h])
+        sibs.append(send(mine(2), mine(2), sib))
+        yield
+        for r, i in zip((0, 3, 1, 2), sibs):
+            got(its(r), i)
+
+    def flow_x():
+        def take(*ks):
+            for k in ks:
+                r = NEAR[k]
+                got(dr.at[rem4(x + r)], to_sib[k])
+                add(xrow(r), [dr.at[rem4(x + r)]])
+
+        yield
+        take(0)
+        ids = far(xrow, xa, xb, at_x)
+        yield
+        take(1, 2)
+        ids += near(xrow, xm, xp, at_x)
+        yield
+        take(3)
+        h_load.wait()
+        ub[...] = mm(hown[...], wt_ref[...]) + row_of(bt_ref)
+        yield from scatter_rest(xrow, xa, xb, xm, xp, at_x, ids)
+        yield
+        scatter_end(xm, xp, ids)
+        layer_back()
+        for i in to_sib:
+            listed[i].wait_send()
+        dwt = dt.at[pl.ds(al(other * HN), D)]
+        for cols in cuts(D):
+            dwt[:, cols] = mm(hown[...], dub[:, cols], TN)
+        i_wr = send(dwt.at[pl.ds(al(other * HD), HD)], wr, sib)
+        vect[tp] = jnp.concatenate([jnp.sum(vec[i], **ROWS) for i in range(GB)], axis=0)
+        ids = [send(vect.at[tp], vect.at[tp], at_t(r)) for r in range(1, 8)]
+        begin("w", flow_w(dwt, i_wr))
+        begin("v", flow_v(ids))
+        for cols in cuts(D):
+            ub[:, cols] = mm(dub[...], wt_ref[cols, :], NTR).astype(BF16).astype(F32)
+
     lb = 64 if NR % 64 == 0 else 16
-    dtown = xrow(0)
-    vec[...] = jnp.zeros_like(vec)
-
-    def back(i, carry):
-        rows = pl.ds(al(i * lb, 16), lb)
-        u = ub[rows, :]
-        cdf = 0.5 * (1.0 + lax.erf(u * RSQRT2))
-        a = u * cdf
-        ctr = a - jnp.mean(a, **COLS)
-        rstd = lax.rsqrt(jnp.mean(ctr * ctr, **COLS) + LN_EPS)
-        xh = ctr * rstd
-        g = dtown[rows, :] + xm[rows, :] + xp[rows, :]
-        gx = g * xh
-        gg = g * gamma
-        m1 = jnp.mean(gg, **COLS)
-        m2 = jnp.mean(gg * xh, **COLS)
-        da = rstd * (gg - m1 - xh * m2)
-        pdf = jnp.exp(u * u * -0.5) * 0.3989422804014327
-        du = da * (cdf + u * pdf)
-        dub[rows, :] = du.astype(BF16)
-        for j, v in enumerate((gx, g, du)):
-            vec[j] += jnp.sum(v.reshape(lb // GB, GB, D), axis=0)
-        return carry
-
-    lax.fori_loop(0, NR // lb, back, 0)
-    listed[to_sib].wait_send()
-    dwt = dt.at[pl.ds(al(other * HN), D)]
-    for cols in cuts(D):
-        dwt[:, cols] = mm(hown[...], dub[:, cols], TN)
-    i_wr = send(dwt.at[pl.ds(al(other * HD), HD)], wr, sib)
-    ag_p[0].begin(fin)
-    vect[tp] = jnp.concatenate([jnp.sum(vec[i], **ROWS) for i in range(GB)], axis=0)
-    ids_t = [send(vect.at[tp], vect.at[tp], at_t(r)) for r in range(1, 8)]
-    for cols in cuts(D):
-        ub[:, cols] = mm(dub[...], wt_ref[cols, :], NTR).astype(BF16).astype(F32)
-
-    def wrow(r, h=ALL):
-        return spot(dwt, core * HD + rem4(x + r) * WR, WR, h)
-
-    rs_w = Scatter(wrow, wxa, wxb, wxm, wxp, at_x)
-    got(wr, i_wr)
-    add(dwt.at[pl.ds(al(core * HD), HD)], [wr])
-    rs_w.begin()
-    ag_q.middle()
-    ag_p[1].begin(orow(0, 3))
-    ag_p[2].begin(orow(0, 1))
-    rs_w.middle()
-
-    def hrow(c):
-        return lambda r, h=ALL: spot(dh_out, (c * 4 + rem4(x + r)) * NR, NR, h)
-
-    ag_h = Gather(hrow(core), at_x, hrow(other))
-    ag_h.begin(ub)
-    keep.append(pltpu.make_async_copy(ub, hrow(core)(0), osem.at[1]))
-    keep[1].start()
-
-    for r, i in zip(range(1, 8), ids_t):
-        got(vect.at[rem8(tp - r)], i)
-    acc = vect[0]
-    for k in range(1, 8):
-        acc = acc + vect[k]
-    vecy[yc] = acc
-    ids_y = share(vecy, yc, at_y)
-
-    rs_w.end()
-    wown = wrow(0)
-    add(wown, [wxm, wxp])
-
-    def piece(ref, k):
-        return ref.at[pl.ds(al(k * WP), WP)]
-
-    ids_q = [send(piece(wown, rem4(q + r)), wq.at[q], at_q(r)) for r in RING]
-    wq[q] = piece(wown, q)[...]
-    ag_q.end()
-    ag_p[3].begin(orow(0, 2))
-    wp[p] = shared(wq, q, ids_q)
-    ids_p = share(wp, p, at_p)
-    ag_p[0].middle()
-    dbo_out[...] = shared(vbz, zc, ids_z)
-    vecz[zc] = shared(vecy, yc, ids_y)
-    ids_z = share(vecz, zc, at_z)
-    piece(wag, q)[...] = shared(wp, p, ids_p)
-    ids_q = [send(piece(wag, q), piece(wag, q), at_q(r)) for r in RING]
-    ag_p[1].middle()
-    for r, i in zip(RING, ids_q):
-        got(piece(wag, rem4(q - r)), i)
-
-    def grow(c):
-        return lambda r, h=ALL: spot(dwt_out, c * HD + rem4(x + r) * WR, WR, h)
-
-    ag_w = Gather(grow(core), at_x, grow(other))
-    ag_w.begin(wag)
-    keep.append(pltpu.make_async_copy(wag, grow(core)(0), osem.at[2]))
-    keep[2].start()
-    ag_h.middle()
-    ag_p[2].middle()
-    vec_out[...] = shared(vecz, zc, ids_z)
-    ag_h.end()
-    ag_w.middle()
-    ag_p[3].middle()
-    ag_w.end()
-
-    ag_h.close()
-    ag_w.close()
-    for g in ag_p:
-        g.end()
+
+    def layer_back():
+        dtown = xrow(0)
+        gamma = row_of(gm_ref)
+        vec[...] = jnp.zeros_like(vec)
+
+        def back(i, carry):
+            rows = pl.ds(al(i * lb, 16), lb)
+            u = ub[rows, :]
+            cdf = 0.5 * (1.0 + lax.erf(u * RSQRT2))
+            a = u * cdf
+            ctr = a - jnp.mean(a, **COLS)
+            rstd = lax.rsqrt(jnp.mean(ctr * ctr, **COLS) + LN_EPS)
+            xh = ctr * rstd
+            g = dtown[rows, :] + xm[rows, :] + xp[rows, :]
+            gx = g * xh
+            gg = g * gamma
+            m1 = jnp.mean(gg, **COLS)
+            m2 = jnp.mean(gg * xh, **COLS)
+            da = rstd * (gg - m1 - xh * m2)
+            pdf = jnp.exp(u * u * -0.5) * 0.3989422804014327
+            du = da * (cdf + u * pdf)
+            dub[rows, :] = du.astype(BF16)
+            for j, v in enumerate((gx, g, du)):
+                vec[j] += jnp.sum(v.reshape(lb // GB, GB, D), axis=0)
+            return carry
+
+        lax.fori_loop(0, NR // lb, back, 0)
+
+    def swapped(src, dst, value):
+        src[...] = value
+        return send(src, dst, sib)
+
+    def flow_w(dwt, i_wr):
+        def wrow(r, h=ALL):
+            return spot(dwt, core * HD + rem4(x + r) * WR, WR, h)
+
+        def piece(ref, k):
+            return ref.at[pl.ds(al(k * WP), WP)]
+
+        yield
+        got(wr, i_wr)
+        add(dwt.at[pl.ds(al(core * HD), HD)], [wr])
+        ids = far(wrow, wxa, wxb, at_x) + near(wrow, wxm, wxp, at_x)
+        yield from scatter_rest(wrow, wxa, wxb, wxm, wxp, at_x, ids)
+        begin("h", gather_x(ub, dh_out, NR))
+        yield
+        scatter_end(wxm, wxp, ids)
+        mine = wrow(0)
+        add(mine, [wxm, wxp])
+        ids = [send(piece(mine, rem4(q + r)), wq.at[q], at_q(r)) for r in RING]
+        wq[q] = piece(mine, q)[...]
+        yield
+        i = swapped(w1, w2, shared(wq, q, ids))
+        yield
+        got(w2, i)
+        wp[q] = w2[...]
+        ids = share(wp, q, at_q)
+        yield
+        i = swapped(w3, w4, shared(wp, q, ids))
+        yield
+        got(w4, i)
+        piece(wag, q)[...] = w4[...]
+        ids = [send(piece(wag, q), piece(wag, q), at_q(r)) for r in RING]
+        yield
+        for r, i in zip(RING, ids):
+            got(piece(wag, rem4(q - r)), i)
+        yield from gather_x(wag, dwt_out, WR)
+
+    def flow_v(ids):
+        yield
+        for r, i in zip(range(1, 8), ids):
+            got(vect.at[rem8(tp - r)], i)
+        vecq[q] = sum(vect[k] for k in range(8))
+        ids = share(vecq, q, at_q)
+        yield
+        i = swapped(v1, v2, shared(vecq, q, ids))
+        yield
+        got(v2, i)
+        vecp[q] = v2[...]
+        ids = share(vecp, q, at_q)
+        yield
+        total = shared(vecp, q, ids)
+        i = swapped(v3, v4, total)
+        yield
+        got(v4, i)
+        vec_out[...] = jnp.where(core == 0, v3[...], v4[...])
+
+    for name, gen in (("p", flow_p()), ("x", flow_x()), ("b", flow_b())):
+        begin(name, gen)
+    for name in STEPS:
+        next(flows[name], 0)
+    for gen in flows.values():
+        assert next(gen, ALL) is ALL and gen.gi_frame is ALL
+
     for cp in keep:
         cp.wait()
     for i, cp in enumerate(listed):
-        if i != to_sib:
+        if i not in to_sib:
             cp.wait_send()
 
 
@@ -724,7 +751,7 @@
     any_ = pl.BlockSpec(memory_space=pl.ANY)
     vm = pl.BlockSpec(memory_space=pltpu.VMEM)
     sd = jax.ShapeDtypeStruct
-    D, BLK, CH, TT, NR, WR = d.D, d.BLK, d.CH, d.TT, d.NR, d.WR
+    D, BLK, TT, NR, WR = d.D, d.BLK, d.TT, d.NR, d.WR
 
     def vf(*shape):
         return pltpu.VMEM((*shape, D), F32)
@@ -741,15 +768,15 @@
     dma = pltpu.SemaphoreType.DMA
     return pl.pallas_call(
         functools.partial(train_kernel, d),
-        out_shape=(sd((d.VP, D), F32), sd((d.N, D), F32), sd((D, D), F32), sd((GB, D), F32), sd((2 * NCH, d.CL), F32)),
+        out_shape=(sd((d.VP, D), F32), sd((d.N, D), F32), sd((D, D), F32), sd((GB, D), F32), sd((3 * GB, d.CL), F32)),
         in_specs=[any_, any_, any_, vm, any_, vm, vm, vm, vm],
         out_specs=(any_, any_, any_, vm, vm),
         scratch_shapes=[
-            vh(d.N, D), vh(2, CH, D), vl(2, NT, CH, TT), vh(2, CH, TT), vf(d.N), vf(16, BLK), *twice(vf(4, BLK)),
-            *twice(vf(d.HB)), *twice(vf(BLK)), vf(d.HN), *twice(vf(d.HR)), *twice(vf(NR)),
-            vf(NR), *twice(vh(NR, D)), vf(d.HD), *twice(vf(WR // 2)), *twice(vf(WR)), *twice(vf(4, d.WP)), vf(WR),
-            vl(8, NT, 8, TT), vl(NT, 8, TT), vl(d.CL, LANES), vl(2 * NCH, d.CL), *twice(vl(4, 2 * NCH, d.CL)),
-            *twice(vl(4, GB, LANES)), *twice(vf(GB, GB)), *twice(vf(4, GB)),
+            vh(d.N, D), vh(2, BLK, D), vl(2, NT, BLK, TT), vh(2, BLK, TT), vf(d.N), vf(16, BLK), *twice(vf(4, BLK)),
+            *twice(vf(d.HB)), *twice(vf(BLK)), vf(4, NR), *twice(vf(d.HR)), *twice(vf(NR)),
+            vf(NR), *twice(vh(NR, D)), vf(d.HD), *twice(vf(WR // 2)), *twice(vf(WR)), *twice(vf(4, d.WP)), *twice(vf(d.WP)), *twice(vf(d.WP)), vf(WR),
+            vl(8, NT, 8, TT), vl(NT, 8, TT), vl(d.CL, LANES), vl(3 * GB, d.CL), *twice(vl(4, 3 * GB, d.CL)),
+            *twice(vl(4, GB, LANES)), *twice(vf(GB, GB)), *twice(vf(4, GB)), *twice(vf(GB)), *twice(vf(GB)),
             dma((2,)), dma((2,)), dma((2, NT)), dma((3,)), *twice(dma((NSEM,))),
         ],
         compiler_params=pltpu.CompilerParams(vmem_limit_bytes=VMEM_MAX, collective_id=0, has_side_effects=True),
@@ -788,7 +815,7 @@
     for row, ref in ((LAB, g_out), (LIVE, b_out), (SRC, t_out)):
         for i, cols in enumerate(cuts(d.D)):
             ref[slice(i, i + 1), :] = vec_ref[row, cols]
-    loss[...] = dbo_ref[NCH:NCH + 1, LAB]
+    loss[...] = dbo_ref[16:17, LAB]
     first.wait()
 
     def group(g, o):
@@ -861,7 +888,7 @@
                                              w_t, bt, gm, be, embed, bias)
         de, dh, dwt, vec, dbo = train(d, t, h, z, meta, e, w_t, bt, gm, be)
         d_hidden, d_embed, d_w, d_gamma, d_beta, d_bt, loss = finish(d, cnt, col, dh, de, dwt, vec, dbo)
-        d_bias = dbo[:NCH, :d.CH].reshape(-1)[:d.V]
+        d_bias = dbo[:16, :d.BLK].reshape(-1)[:d.V]
         return (loss.reshape(()), d_hidden.reshape(hidden.shape), d_w, d_bt.reshape(-1), d_gamma.reshape(-1),
                 d_beta.reshape(-1), d_embed, d_bias)
 

time: 260 us -> 229 us (0.88); the launches traced: 258 us -> 231 us
  Pallas kernels: 255 us -> 228 us
    pallas_call x1, Pallas kernels: 187 us -> 166 us  [train(): pl.pallas_call(functools.partial(train_kernel, d), out_shape=(sd((d.VP, D...]
    pallas_call x1, Pallas kernels: 42.6 us -> 36.1 us  [forward(): pl.pallas_call(functools.partial(forward_kernel, d), out_shape=(sd((d.N,...]
where the time goes in v2:
time: 229 us; the launch traced here: 231 us
  Pallas kernels  228 us (100%)
  local copies, waits for them, and re-layouts  2.74 us (1%)
    pallas_call x1, Pallas kernels, train(): pl.pallas_call(functools.partial(train_kernel, d), out_shape=(sd((d.VP, D...  166 us
    pallas_call x1, Pallas kernels, forward(): pl.pallas_call(functools.partial(forward_kernel, d), out_shape=(sd((d.N,...  36.1 us
    pallas_call x1, Pallas kernels, finish(): pl.pallas_call(functools.partial(finish_kernel, d), out_shape=(sd((d.B *...  25.2 us

profile of v2, /device:TPU:1, one launch (start us, length us, event | category | flops | bytes accessed | tf_op | source)
XLA Modules:
  0.0 231.2 jit_solution(15845784211476730224)
XLA Ops:
  0.6 1.3 pad_bitcast_fusion.bias_ref
  2.0 36.1 %mlm_forward.1 = (bf16[2560,768]{1,0:T(8,128)(2,1)}, bf16[2560,768]{1,0:T(8,128)(2,1)}, f32[5,3840,512]{2,1,0:T(8,128)}, f32[5,8,512]{2,1,0:T(8,128)}, f32[2560,...) custom-call(bf16[16384,768]{1,0:T(8,128)(2,1)} %bitcast.15, s32[20,128]{1,0:T(8,128)} %bitcast.23, ...), custom_call_target="tpu_custom_call" | custom-call | tf_op jit(solution)/shard_map/mlm_forward/pallas_call | solution.py:230
  38.0 166.4 %mlm_train.1 = (f32[3840,768]{1,0:T(8,128)}, f32[2560,768]{1,0:T(8,128)}, f32[768,768]{1,0:T(8,128)}, f32[8,768]{1,0:T(8,128)}, f32[24,256]{1,0:T(8,128)}) custom-call(bf16[2560,768]{1,0:T(8,128)(2,1)} %get-tuple-element.29.t_hbm, bf16[2560,768]{1,0:T(8,128)(2,1)} %get-tuple-element.30.h_hbm, f32[5,3840,512]{2,1,0:T(8,128)} %get-tuple-element.31.z_hbm, ...), custom_call_target="tpu_custom_call" | custom-call | tf_op jit(solution)/shard_map/mlm_train/pallas_call | solution.py:769
  204.4 0.7 slice.6
  205.1 0.7 reshape.59
  205.8 25.2 %mlm_finish.1 = (bf16[16384,768]{1,0:T(8,128)(2,1)}, f32[3824,768]{1,0:T(8,128)}, f32[768,768]{1,0:T(8,128)}, f32[6,128]{1,0:T(8,128)}, f32[6,128]{1,0:T(8,128)}, /*index=5*/f32[6,128]{1,0:T(8,128)}, f32[1,1]{1,0:T(1,128)}) custom-call(s32[8,128]{1,0:T(8,128)} %get-tuple-element.27.cnt_hbm, f32[2560,128]{1,0:T(8,128)} %get-tuple-element.28.col_hbm, ...), custom_call_target="tpu_custom_call" | custom-call | tf_op jit(solution)/shard_map/mlm_finish/pallas_call | solution.py:867

commit v3 on v2

--- a/solution.py
+++ b/solution.py
@@ -63,7 +63,7 @@
 
 def forward_kernel(d, h_hbm, idx_ref, lab_ref, w_ref, wt_ref, bt_ref, gm_ref, be_ref, e_hbm, bias_ref,
                    h_out, t_out, z_out, meta_out, col_out, e_out, cnt_out,
-                   hin, hb, tb, ub, eb, bcol, zb, col, meta, keys, cntv, cnt, par3, hsem, esem, zsem, osem):
+                   hin, hb, tb, ub, eb, bcol, zb, col, meta, keys, cntv, cnt, par3, hot_a, hot_b, zero, hsem, esem, zsem, tsem, fsem, osem):
     rows_g = GB * d.L
     tail = d.V - (NCH - 1) * d.CH
 
@@ -83,9 +83,9 @@
     to_smem = pltpu.make_async_copy(cntv, cnt, osem.at[5])
     to_smem.start()
     outs = [pltpu.make_async_copy(a, b, osem.at[i])
-            for i, (a, b) in enumerate(((hb, h_out), (col, col_out), (eb, e_out), (tb, t_out), (meta, meta_out)))]
+            for i, (a, b) in enumerate(((hb, h_out), (col, col_out), (eb, e_out), (meta, meta_out)))]
     outs.append(pltpu.make_async_copy(cntv, cnt_out, osem.at[6]))
-    outs[5].start()
+    outs[4].start()
 
     key = lab_ref[...] * 2048 + idx_ref[...] + 1
     keys[...] = jnp.concatenate([key, jnp.zeros((LANES - d.P, d.B), I32)], axis=0).T
@@ -108,8 +108,7 @@
     p_iota = lax.broadcasted_iota(I32, (1, LANES), 1)
     src_iota = lax.broadcasted_iota(I32, (d.S, rows_g), 1)
 
-    def group(g, o):
-        slot = lax.rem(g, NBUF)
+    def pick(g, hot):
         off = jnp.int32(0)
         key = jnp.zeros((d.S, LANES), I32)
         for j in range(GB):
@@ -120,20 +119,29 @@
             off = off + n_j
         src = jnp.sum((key & 2047).astype(F32), **COLS)
         lab = jnp.sum((key >> 11).astype(F32), **COLS)
-        hot = (src_iota == src.astype(I32) - 1).astype(BF16)
-        h_copy(g, slot).wait()
-        o = pl.multiple_of(o, 16)
-        hb[pl.ds(o, d.S), :] = mm(hot, hin[slot]).astype(BF16)
+        hot[...] = (src_iota == src.astype(I32) - 1).astype(BF16)
         live = (src > 0).astype(F32)
-        col[pl.ds(o, d.S), :] = jnp.where(lane == 0, lab, jnp.where(lane == 1, live, src - 1))
-
-        @pl.when(g + NBUF < d.G)
-        def _():
-            h_copy(g + NBUF, slot).start()
-
-        return o + ((off + 15) // 16) * 16
-
-    used = lax.fori_loop(0, d.G, group, jnp.int32(0))
+        return off, jnp.where(lane == 0, lab, jnp.where(lane == 1, live, src - 1))
+
+    def pair(i, carry):
+        o, n, cols = carry
+        for k, (hot, nxt) in enumerate(((hot_a, hot_b), (hot_b, hot_a))):
+            g = 2 * i + k
+            slot = lax.rem(g, NBUF)
+            h_copy(g, slot).wait()
+            o = pl.multiple_of(o, 16)
+            hb[pl.ds(o, d.S), :] = mm(hot[...], hin[slot]).astype(BF16)
+            col[pl.ds(o, d.S), :] = cols
+            o = o + ((n + 15) // 16) * 16
+            n, cols = pick(jnp.minimum(g + 1, d.G - 1), nxt)
+
+            @pl.when(g + NBUF < d.G)
+            def _():
+                h_copy(g + NBUF, slot).start()
+
+        return o, n, cols
+
+    used, _, _ = lax.fori_loop(0, d.G // 2, pair, (jnp.int32(0), *pick(0, hot_a)))
     tiles = (used + d.TT - 1) // d.TT
     outs[0].start()
     outs[1].start()
@@ -142,82 +150,116 @@
     outs[2].start()
 
     base_v = lax.axis_index("tp") * d.V
-    sub = lax.broadcasted_iota(I32, (8, d.TT), 0)
-    rb = min(128, d.TT)
+    sub = lax.broadcasted_iota(I32, (GB, LANES), 0)
+    rb = min(LANES, d.TT)
+    reps = d.TT // LANES
 
     def z_copy(n, c):
-        return pltpu.make_async_copy(zb.at[lax.rem(n, 2), c], z_out.at[n, pl.ds(c * d.CH, d.CH)],
-                                     zsem.at[lax.rem(n, 2), c])
+        par = lax.rem(n, 2)
+        return pltpu.make_async_copy(zb.at[par, c], z_out.at[n, pl.ds(c * d.CH, d.CH)], zsem.at[par, c])
+
+    def z_fill(n, c):
+        return pltpu.make_async_copy(zero, z_out.at[n, pl.ds(c * d.CH, d.CH)], fsem.at[n, c])
+
+    def fill(n, carry):
+        for c in range(NCH):
+            z_fill(n, c).start()
+        return carry
+
+    zero[...] = jnp.zeros_like(zero)
+    lax.fori_loop(tiles, NT, fill, 0)
+
+    def t_copy(n):
+        rows = pl.ds(pl.multiple_of(n * d.TT, d.TT), d.TT)
+        return pltpu.make_async_copy(tb.at[rows], t_out.at[rows], tsem.at[n])
+
+    def dense(n):
+        ub[...] = mm(hb[pl.ds(pl.multiple_of(n * d.TT, d.TT), d.TT), :], wt_ref[...]) + par3[LAB, :]
+
+    def norm(n, i):
+        u = ub[i * rb:(i + 1) * rb, :]
+        a = 0.5 * u * (1 + lax.erf(u * RSQRT2))
+        ctr = a - jnp.mean(a, **COLS)
+        var = jnp.mean(ctr * ctr, **COLS)
+        t = ctr * lax.rsqrt(var + LN_EPS) * par3[LIVE, :] + par3[SRC, :]
+        tb[pl.ds(pl.multiple_of(n * d.TT + i * rb, rb), rb), :] = t.astype(BF16)
+
+    def wide(v):
+        return jnp.concatenate([v] * reps, axis=1)
+
+    def product(n, c):
+        rows = slice(c * d.CH, (c + 1) * d.CH)
+        t_n = tb[pl.ds(pl.multiple_of(n * d.TT, d.TT), d.TT), :]
+        z = mm(eb[rows, :], t_n, NTR) + wide(bcol[rows, :])
+        zb[lax.rem(n, 2), c] = z
+        mx = jnp.max(z.reshape(d.CH // GB, GB, d.TT), axis=0)
+        return jnp.broadcast_to(jnp.max(mx, **ROWS), (GB, d.TT))
 
     def tile(n, carry):
         par = lax.rem(n, 2)
         base = pl.multiple_of(n * d.TT, d.TT)
+        after = jnp.minimum(n + 1, NT - 1)
+        t_copy(n).start()
 
         @pl.when(n >= 2)
         def _():
             for c in range(NCH):
                 z_copy(n, c).wait()
 
-        ub[...] = mm(hb[pl.ds(base, d.TT), :], wt_ref[...]) + par3[LAB, :]
-
-        def norm(i, carry):
-            r = pl.multiple_of(i * rb, rb)
-            u = ub[pl.ds(r, rb), :]
-            a = 0.5 * u * (1.0 + lax.erf(u * RSQRT2))
-            ctr = a - jnp.mean(a, **COLS)
-            var = jnp.mean(ctr * ctr, **COLS)
-            t = ctr * lax.rsqrt(var + LN_EPS) * par3[LIVE, :] + par3[SRC, :]
-            tb[pl.ds(base + r, rb), :] = t.astype(BF16)
-            return carry
-
-        lax.fori_loop(0, d.TT // rb, norm, 0)
         for cols in cuts(d.TT):
             blk = col[pl.ds(base + cols.start, LANES), :].T
             meta[n, :3, cols] = blk[:3, :]
-
-        t_n = tb[pl.ds(base, d.TT), :]
         lab = meta[n, LAB, :].astype(I32) - base_v
-        lab8 = jnp.broadcast_to(jnp.where(lab < d.V, lab, -1), (8, d.TT))
-        m8 = jnp.full((8, d.TT), -jnp.inf, F32)
-        s8 = jnp.zeros((8, d.TT), F32)
-        t8 = jnp.zeros((8, d.TT), F32)
-        reps = d.TT // LANES
-
-        def product(c):
-            z = mm(eb[c * d.CH:(c + 1) * d.CH, :], t_n, NTR)
-            b = bcol[c * d.CH:(c + 1) * d.CH, :]
-            z = z + jnp.concatenate([b] * reps, axis=1)
-            zb[par, c] = z
-            mx = jnp.max(z.reshape(d.CH // 8, 8, d.TT), axis=0)
-            return jnp.broadcast_to(jnp.max(mx, **ROWS), (8, d.TT))
-
-        nxt = product(0)
+        lab8 = jnp.broadcast_to(jnp.where(lab < d.V, lab, -1), (GB, d.TT))
+        m8 = jnp.full((GB, d.TT), -jnp.inf, F32)
+        s8 = jnp.zeros((GB, d.TT), F32)
+        t8 = jnp.zeros((GB, d.TT), F32)
+        nxt = product(n, 0)
+        dense(after)
         for c in range(NCH):
             z_copy(n, c).start()
             mx = jnp.maximum(m8, nxt)
             if c + 1 < NCH:
-                nxt = product(c + 1)
+                nxt = product(n, c + 1)
             s8 = s8 * jnp.exp(m8 - mx)
             m8 = mx
-            for i in range(d.CH // 8):
-                zz = zb[par, c, i * 8:(i + 1) * 8, :]
-                s8 = s8 + jnp.exp(zz - m8)
-                t8 = t8 + jnp.where(sub + (c * d.CH + i * 8) == lab8, zz, 0.0)
+            zz = zb[par, c].reshape(d.CH // GB, GB, d.TT)
+            s8 = s8 + jnp.sum(jnp.exp(zz - m8[None]), axis=0)
+            at = lax.broadcasted_iota(I32, zz.shape, 0) * GB + lax.broadcasted_iota(I32, zz.shape, 1) + c * d.CH
+            t8 = t8 + jnp.sum(jnp.where(at == lab8[None], zz, 0.0), axis=0)
+            if c >= 4 and c - 4 < d.TT // rb:
+                norm(after, c - 4)
         meta[n, MAX, :] = m8[LAB, :]
         meta[n, SUM, :] = jnp.sum(s8, **ROWS)
         meta[n, TGT, :] = jnp.sum(t8, **ROWS)
         return carry
 
+    dense(0)
+    for i in range(d.TT // rb):
+        norm(0, i)
     lax.fori_loop(0, tiles, tile, 0)
     outs[3].start()
-    outs[4].start()
-
+
+    def rest(n, carry):
+        t_copy(n).start()
+        return carry
+
+    lax.fori_loop(tiles, NT, rest, 0)
     def drain(n, carry):
         for c in range(NCH):
             z_copy(n, c).wait()
         return carry
 
     lax.fori_loop(jnp.maximum(tiles - 2, 0), tiles, drain, 0)
+
+    def filled(n, carry):
+        for c in range(NCH):
+            z_fill(n, c).wait()
+        return carry
+
+    lax.fori_loop(tiles, NT, filled, 0)
+    for n in range(NT):
+        t_copy(n).wait()
     for cp in outs:
         cp.wait()
 
@@ -247,7 +289,10 @@
             pltpu.VMEM((8, d.B), I32),
             pltpu.SMEM((8, d.B), I32),
             pltpu.VMEM((8, d.D), F32),
-            dma((NBUF,)), dma((NCH,)), dma((2, NCH)), dma((7,)),
+            pltpu.VMEM((d.S, GB * d.L), BF16),
+            pltpu.VMEM((d.S, GB * d.L), BF16),
+            pltpu.VMEM((d.CH, d.TT), F32),
+            dma((NBUF,)), dma((NCH,)), dma((2, NCH)), dma((NT,)), dma((NT, NCH)), dma((7,)),
         ],
         compiler_params=pltpu.CompilerParams(vmem_limit_bytes=VMEM_MAX),
         name="mlm_forward",
@@ -425,7 +470,7 @@
     ce = jnp.sum(ce, **COLS) / denom
     t_load.wait()
 
-    sub = lax.broadcasted_iota(I32, (16, TT), 0)
+    sub = lax.broadcasted_iota(I32, (16, LANES), 0)
     row16 = lax.broadcasted_iota(I32, (16, LANES), 0)
     dacc[BLK:, :] = jnp.zeros((d.CL - BLK, LANES), F32)
 
@@ -434,12 +479,11 @@
         a8 = jnp.broadcast_to(comb[n, LIVE, :], (16, TT))
         c8 = jnp.broadcast_to(comb[n, SRC, :], (16, TT))
         l8 = jnp.broadcast_to(comb[n, MAX, :].astype(I32) - cid * BLK, (16, TT))
-        live = c8 > 0
         for i in range(BLK // 16):
             rows = slice(i * 16, (i + 1) * 16)
             g = jnp.exp(zb[slot, n, rows, :] - m8) * a8
-            g = g - jnp.where(sub + i * 16 == l8, c8, 0.0)
-            g = jnp.where(live, g, 0.0)
+            at = jnp.concatenate([sub + i * 16] * (TT // LANES), axis=1)
+            g = g - jnp.where(at == l8, c8, 0.0)
             dzb[n % 2, rows, :] = g.astype(BF16)
             part = sum(g[:, cols] for cols in cuts(TT))
             dacc[rows, :] = part if n == 0 else dacc[rows, :] + part
@@ -786,7 +830,7 @@
 
 def finish_kernel(d, cnt_hbm, col_hbm, dh_hbm, de_hbm, dwt_hbm, vec_ref, dbo_ref,
                   dH, dE, dW, g_out, b_out, t_out, loss,
-                  cnt, colb, dhb, stage, wstage, outb, isem, csem, osem, dsem, esem, ssem):
+                  cnt, colb, dhb, stage, wstage, outb, isem, osem, dsem, esem, ssem):
     rows_g = GB * d.L
     src_iota = lax.broadcasted_iota(I32, (d.S, rows_g), 1)
     r_iota = lax.broadcasted_iota(I32, (d.S, 1), 0)
@@ -800,47 +844,40 @@
     ins.append(pltpu.make_async_copy(dwt_hbm, wstage, dsem.at[NCH]))
     outs.append(pltpu.make_async_copy(wstage, dW, esem.at[NCH]))
 
-    def loads(o, slot):
-        o = pl.multiple_of(o, 16)
-        return [pltpu.make_async_copy(dh_hbm.at[pl.ds(o, d.S)], dhb.at[slot], isem.at[slot]),
-                pltpu.make_async_copy(col_hbm.at[pl.ds(o, d.S)], colb.at[slot], csem.at[slot])]
+    rows_h = [pltpu.make_async_copy(dh_hbm.at[pl.ds(c * d.NR, d.NR)], dhb.at[pl.ds(c * d.NR, d.NR)], isem.at[c])
+              for c in range(NCH)]
+    rows_h.append(pltpu.make_async_copy(col_hbm, colb, isem.at[NCH]))
 
     def out_copy(g, slot):
         return pltpu.make_async_copy(outb.at[slot], dH.at[pl.ds(g * rows_g, rows_g)], osem.at[slot])
 
-    for cp in loads(jnp.int32(0), 0):
-        cp.start()
-    for cp in ins:
+    for cp in rows_h[NCH:] + rows_h[:2] + ins[:2] + rows_h[2:NCH] + ins[2:]:
         cp.start()
     for row, ref in ((LAB, g_out), (LIVE, b_out), (SRC, t_out)):
         for i, cols in enumerate(cuts(d.D)):
             ref[slice(i, i + 1), :] = vec_ref[row, cols]
     loss[...] = dbo_ref[16:17, LAB]
     first.wait()
+    rows_h[NCH].wait()
 
     def group(g, o):
-        slot = lax.rem(g, 2)
         oslot = lax.rem(g, NBUF)
         c = cnt[0, g * GB]
         for j in range(1, GB):
             c = c + cnt[0, g * GB + j]
-        nxt = o + ((c + 15) // 16) * 16
-
-        @pl.when(g + 1 < d.G)
-        def _():
-            for cp in loads(nxt, 1 - slot):
-                cp.start()
-
-        for cp in loads(o, slot):
-            cp.wait()
+        o = pl.multiple_of(o, 16)
+        for i in range(NCH):
+            @pl.when(g == i * (d.G // NCH))
+            def _(i=i):
+                rows_h[i].wait()
 
         @pl.when(g >= NBUF)
         def _():
             out_copy(g - NBUF, oslot).wait()
 
-        src = jnp.where(r_iota < c, colb[slot, :, SRC].astype(I32), -1)
+        src = jnp.where(r_iota < c, colb[pl.ds(o, d.S), SRC].astype(I32), -1)
         hot = (src_iota == src).astype(BF16)
-        outb[oslot] = mm(hot, dhb[slot].astype(BF16), TN).astype(BF16)
+        outb[oslot] = mm(hot, dhb[pl.ds(o, d.S), :].astype(BF16), TN).astype(BF16)
         out_copy(g, oslot).start()
 
         for i, (a, b) in enumerate(zip(ins, outs)):
@@ -849,7 +886,7 @@
                 a.wait()
                 b.start()
 
-        return nxt
+        return o + ((c + 15) // 16) * 16
 
     lax.fori_loop(0, d.G, group, jnp.int32(0))
     for g in range(d.G - NBUF, d.G):
@@ -870,9 +907,9 @@
         in_specs=[any_, any_, any_, any_, any_, vm, vm],
         out_specs=(any_, any_, any_, vm, vm, vm, vm),
         scratch_shapes=[
-            pltpu.SMEM((GB, d.B), I32), pltpu.VMEM((2, d.S, LANES), F32), pltpu.VMEM((2, d.S, d.D), F32),
+            pltpu.SMEM((GB, d.B), I32), pltpu.VMEM((d.N, LANES), F32), pltpu.VMEM((d.N, d.D), F32),
             pltpu.VMEM((d.VP, d.D), F32), pltpu.VMEM((d.D, d.D), F32), pltpu.VMEM((NBUF, GB * d.L, d.D), BF16),
-            dma((2,)), dma((2,)), dma((NBUF,)), dma((NCH + 1,)), dma((NCH + 1,)), dma((1,)),
+            dma((NCH + 1,)), dma((NBUF,)), dma((NCH + 1,)), dma((NCH + 1,)), dma((1,)),
         ],
         compiler_params=pltpu.CompilerParams(vmem_limit_bytes=VMEM_MAX),
         name="mlm_finish",

time: 229 us -> 224 us (0.978); the launches traced: 231 us -> 221 us
  Pallas kernels: 228 us -> 217 us
    pallas_call x1, Pallas kernels: 166 us -> 159 us  [train(): pl.pallas_call(functools.partial(train_kernel, d), out_shape=(sd((d.VP, D...]
    pallas_call x1, Pallas kernels: 36.1 us -> 33 us  [forward(): pl.pallas_call(functools.partial(forward_kernel, d), out_shape=(sd((d.N,...]
where the time goes in v3:
time: 224 us; the launch traced here: 221 us
  Pallas kernels  217 us (97%)
  local copies, waits for them, and re-layouts  2.74 us (1%)
    pallas_call x1, Pallas kernels, train(): pl.pallas_call(functools.partial(train_kernel, d), out_shape=(sd((d.VP, D...  159 us
    pallas_call x1, Pallas kernels, forward(): pl.pallas_call(functools.partial(forward_kernel, d), out_shape=(sd((d.N,...  33 us
    pallas_call x1, Pallas kernels, finish(): pl.pallas_call(functools.partial(finish_kernel, d), out_shape=(sd((d.B *...  24.7 us

profile of v3, /device:TPU:1, one launch (start us, length us, event | category | flops | bytes accessed | tf_op | source)
XLA Modules:
  0.0 220.7 jit_solution(7712948931659627637)
XLA Ops:
  0.6 1.3 pad_bitcast_fusion.bias_ref
  2.0 33.0 %mlm_forward.1 = (bf16[2560,768]{1,0:T(8,128)(2,1)}, bf16[2560,768]{1,0:T(8,128)(2,1)}, f32[5,3840,512]{2,1,0:T(8,128)}, f32[5,8,512]{2,1,0:T(8,128)}, f32[2560,...) custom-call(bf16[16384,768]{1,0:T(8,128)(2,1)} %bitcast.15, s32[20,128]{1,0:T(8,128)} %bitcast.23, ...), custom_call_target="tpu_custom_call" | custom-call | tf_op jit(solution)/shard_map/mlm_forward/pallas_call | solution.py:272
  35.0 159.4 %mlm_train.1 = (f32[3840,768]{1,0:T(8,128)}, f32[2560,768]{1,0:T(8,128)}, f32[768,768]{1,0:T(8,128)}, f32[8,768]{1,0:T(8,128)}, f32[24,256]{1,0:T(8,128)}) custom-call(bf16[2560,768]{1,0:T(8,128)(2,1)} %get-tuple-element.29.t_hbm, bf16[2560,768]{1,0:T(8,128)(2,1)} %get-tuple-element.30.h_hbm, f32[5,3840,512]{2,1,0:T(8,128)} %get-tuple-element.31.z_hbm, ...), custom_call_target="tpu_custom_call" | custom-call | tf_op jit(solution)/shard_map/mlm_train/pallas_call | solution.py:813
  194.4 0.7 slice.6
  195.1 0.7 reshape.59
  195.8 24.7 %mlm_finish.1 = (bf16[16384,768]{1,0:T(8,128)(2,1)}, f32[3824,768]{1,0:T(8,128)}, f32[768,768]{1,0:T(8,128)}, f32[6,128]{1,0:T(8,128)}, f32[6,128]{1,0:T(8,128)}, /*index=5*/f32[6,128]{1,0:T(8,128)}, f32[1,1]{1,0:T(1,128)}) custom-call(s32[8,128]{1,0:T(8,128)} %get-tuple-element.27.cnt_hbm, f32[2560,128]{1,0:T(8,128)} %get-tuple-element.28.col_hbm, ...), custom_call_target="tpu_custom_call" | custom-call | tf_op jit(solution)/shard_map/mlm_finish/pallas_call | solution.py:904

commit v4 on v3

--- a/solution.py
+++ b/solution.py
@@ -53,6 +53,10 @@
         self.CL = -(-self.BLK // LANES) * LANES
 
 
+def up16(n):
+    return (n + 15) // 16 * 16
+
+
 def cuts(n):
     return [slice(i, min(i + LANES, n)) for i in range(0, n, LANES)]
 
@@ -62,8 +66,8 @@
 
 
 def forward_kernel(d, h_hbm, idx_ref, lab_ref, w_ref, wt_ref, bt_ref, gm_ref, be_ref, e_hbm, bias_ref,
-                   h_out, t_out, z_out, meta_out, col_out, e_out, cnt_out,
-                   hin, hb, tb, ub, eb, bcol, zb, col, meta, keys, cntv, cnt, par3, hot_a, hot_b, zero, hsem, esem, zsem, tsem, fsem, osem):
+                   h_out, t_out, z_out, meta_out, col_out, cnt_out,
+                   hin, hb, tb, ub, eb, bcol, zb, col, meta, keys, cntv, cnt, par3, hot_a, hot_b, hsem, esem, zsem, tsem, osem):
     rows_g = GB * d.L
     tail = d.V - (NCH - 1) * d.CH
 
@@ -76,16 +80,15 @@
 
     for g in range(NBUF):
         h_copy(g, g).start()
-    for c in range(NCH):
-        e_copy(c).start()
 
     cntv[...] = jnp.broadcast_to(jnp.sum(w_ref[...], **ROWS), cntv.shape).astype(I32)
-    to_smem = pltpu.make_async_copy(cntv, cnt, osem.at[5])
+    to_smem = pltpu.make_async_copy(cntv, cnt, osem.at[0])
     to_smem.start()
-    outs = [pltpu.make_async_copy(a, b, osem.at[i])
-            for i, (a, b) in enumerate(((hb, h_out), (col, col_out), (eb, e_out), (meta, meta_out)))]
-    outs.append(pltpu.make_async_copy(cntv, cnt_out, osem.at[6]))
-    outs[4].start()
+    tp = lax.axis_index("tp")
+    mine = pl.ds(pl.multiple_of((lax.rem(tp, 2) * 4 + tp // 2) * d.NR, 16), d.NR)
+    pairs = (cntv, cnt_out), (hb.at[mine], h_out), (col, col_out), (meta, meta_out)
+    outs = [pltpu.make_async_copy(a, b, osem.at[i + 1]) for i, (a, b) in enumerate(pairs)]
+    outs[0].start()
 
     key = lab_ref[...] * 2048 + idx_ref[...] + 1
     keys[...] = jnp.concatenate([key, jnp.zeros((LANES - d.P, d.B), I32)], axis=0).T
@@ -125,6 +128,12 @@
 
     def pair(i, carry):
         o, n, cols = carry
+
+        @pl.when(i == 1)
+        def _():
+            for c in range(NCH):
+                e_copy(c).start()
+
         for k, (hot, nxt) in enumerate(((hot_a, hot_b), (hot_b, hot_a))):
             g = 2 * i + k
             slot = lax.rem(g, NBUF)
@@ -132,7 +141,7 @@
             o = pl.multiple_of(o, 16)
             hb[pl.ds(o, d.S), :] = mm(hot[...], hin[slot]).astype(BF16)
             col[pl.ds(o, d.S), :] = cols
-            o = o + ((n + 15) // 16) * 16
+            o = o + up16(n)
             n, cols = pick(jnp.minimum(g + 1, d.G - 1), nxt)
 
             @pl.when(g + NBUF < d.G)
@@ -143,13 +152,12 @@
 
     used, _, _ = lax.fori_loop(0, d.G // 2, pair, (jnp.int32(0), *pick(0, hot_a)))
     tiles = (used + d.TT - 1) // d.TT
-    outs[0].start()
-    outs[1].start()
+    for cp in outs[1:3]:
+        cp.start()
     for c in range(NCH):
         e_copy(c).wait()
-    outs[2].start()
-
-    base_v = lax.axis_index("tp") * d.V
+
+    base_v = tp * d.V
     sub = lax.broadcasted_iota(I32, (GB, LANES), 0)
     rb = min(LANES, d.TT)
     reps = d.TT // LANES
@@ -157,17 +165,6 @@
     def z_copy(n, c):
         par = lax.rem(n, 2)
         return pltpu.make_async_copy(zb.at[par, c], z_out.at[n, pl.ds(c * d.CH, d.CH)], zsem.at[par, c])
-
-    def z_fill(n, c):
-        return pltpu.make_async_copy(zero, z_out.at[n, pl.ds(c * d.CH, d.CH)], fsem.at[n, c])
-
-    def fill(n, carry):
-        for c in range(NCH):
-            z_fill(n, c).start()
-        return carry
-
-    zero[...] = jnp.zeros_like(zero)
-    lax.fori_loop(tiles, NT, fill, 0)
 
     def t_copy(n):
         rows = pl.ds(pl.multiple_of(n * d.TT, d.TT), d.TT)
@@ -252,12 +249,6 @@
 
     lax.fori_loop(jnp.maximum(tiles - 2, 0), tiles, drain, 0)
 
-    def filled(n, carry):
-        for c in range(NCH):
-            z_fill(n, c).wait()
-        return carry
-
-    lax.fori_loop(tiles, NT, filled, 0)
     for n in range(NT):
         t_copy(n).wait()
     for cp in outs:
@@ -271,10 +262,10 @@
     dma = pltpu.SemaphoreType.DMA
     return pl.pallas_call(
         functools.partial(forward_kernel, d),
-        out_shape=(sd((d.N, d.D), BF16), sd((d.N, d.D), BF16), sd((NT, d.VP, d.TT), F32), sd((NT, 8, d.TT), F32),
-                   sd((d.N, LANES), F32), sd((d.VP, d.D), BF16), sd((8, d.B), I32)),
+        out_shape=(sd((d.NR, d.D), BF16), sd((d.N, d.D), BF16), sd((NT, d.VP, d.TT), F32), sd((NT, 8, d.TT), F32),
+                   sd((d.N, LANES), F32), sd((8, d.B), I32)),
         in_specs=[any_, vm, vm, vm, vm, vm, vm, vm, any_, vm],
-        out_specs=(any_,) * 7,
+        out_specs=(any_,) * 6,
         scratch_shapes=[
             pltpu.VMEM((NBUF, GB * d.L, d.D), BF16),
             pltpu.VMEM((d.N, d.D), BF16),
@@ -291,8 +282,7 @@
             pltpu.VMEM((8, d.D), F32),
             pltpu.VMEM((d.S, GB * d.L), BF16),
             pltpu.VMEM((d.S, GB * d.L), BF16),
-            pltpu.VMEM((d.CH, d.TT), F32),
-            dma((NBUF,)), dma((NCH,)), dma((2, NCH)), dma((NT,)), dma((NT, NCH)), dma((7,)),
+            dma((NBUF,)), dma((NCH,)), dma((2, NCH)), dma((NT,)), dma((5,)),
         ],
         compiler_params=pltpu.CompilerParams(vmem_limit_bytes=VMEM_MAX),
         name="mlm_forward",
@@ -301,6 +291,7 @@
 
 MESH = pl.DeviceIdType.MESH
 RING = (1, 2, 3)
+OTHERS = range(1, 8)
 NSEM = 128
 NEAR = (2, 1, 3, 0)
 CODES = "200210201211110300111301100310101311000010001011"
@@ -410,21 +401,39 @@
             out = jnp.where(k == i, rem4(p + rel) * 4 + b, out)
         return out
 
-    def loads(k):
+    last = d.VP // BLK - 1
+    tail = d.V - last * BLK
+
+    def loads(k, act):
         slot = lax.rem(k, 2)
-        r = block_id(k) * BLK
-        return [pltpu.make_async_copy(e_hbm.at[pl.ds(al(r, 16), BLK)], eb.at[slot], esem.at[slot])] + [
-            pltpu.make_async_copy(z_hbm.at[n, pl.ds(al(r), BLK)], zb.at[slot, n], zsem.at[slot, n]) for n in range(NT)]
-
+        b = block_id(k)
+        r = b * BLK
+        for n in range(NT):
+            act(pltpu.make_async_copy(z_hbm.at[n, pl.ds(al(r), BLK)], zb.at[slot, n], zsem.at[slot, n]))
+
+        @pl.when(b < last)
+        def _():
+            act(pltpu.make_async_copy(e_hbm.at[pl.ds(al(r, 16), BLK)], eb.at[slot], esem.at[slot]))
+
+        @pl.when(b == last)
+        def _():
+            act(pltpu.make_async_copy(e_hbm.at[pl.ds(last * BLK, tail)], eb.at[slot, pl.ds(0, tail)], esem.at[slot]))
+
+    def start(cp):
+        cp.start()
+
+    def wait(cp):
+        cp.wait()
+
+    eb[...] = jnp.zeros_like(eb)
+    loads(jnp.int32(0), start)
     t_load = pltpu.make_async_copy(t_hbm, tb, lsem.at[0])
-    h_load = pltpu.make_async_copy(h_hbm.at[pl.ds(al((core * 4 + x) * NR, 16), NR)], hown, lsem.at[1])
-    for cp in loads(jnp.int32(0)):
-        cp.start()
+    h_load = pltpu.make_async_copy(h_hbm, hown, lsem.at[1])
     t_load.start()
     h_load.start()
 
     barrier = pltpu.get_barrier_semaphore()
-    peers = [f(r) for f in (at_y, at_z) for r in RING] + [at_t(r) for r in range(1, 8)]
+    peers = [f(r) for f in (at_y, at_z) for r in RING] + [at_t(r) for r in OTHERS]
     for dev in peers:
         pl.semaphore_signal(barrier, inc=1, device_id=dev, device_id_type=MESH)
     wsum = jnp.zeros((1, 1), F32)
@@ -435,19 +444,19 @@
     pl.semaphore_wait(barrier, len(peers))
 
     ids_y = share(dnp, yc, at_y)
-    ids_t = [send(meta, srecv.at[tp], at_t(r)) for r in range(1, 8)]
+    ids_t = [send(meta, srecv.at[tp], at_t(r)) for r in OTHERS]
     dt[...] = jnp.zeros_like(dt)
     for k in (*range(8), *range(12, 16)):
         de[k] = jnp.zeros((BLK, D), F32)
     vb[...] = jnp.zeros_like(vb)
     dnq[zc] = shared(dnp, yc, ids_y)
     ids_z = share(dnq, zc, at_z)
-    for r, i in zip(range(1, 8), ids_t):
+    for r, i in zip(OTHERS, ids_t):
         got(srecv.at[rem8(tp - r)], i)
     tiles = []
     for n in range(NT):
         mx = srecv[0, n, MAX, :]
-        for k in range(1, 8):
+        for k in OTHERS:
             mx = jnp.maximum(mx, srecv[k, n, MAX, :])
         tot = jnp.zeros((1, TT), F32)
         tgt = jnp.zeros((1, TT), F32)
@@ -478,12 +487,15 @@
         m8 = jnp.broadcast_to(comb[n, LAB, :], (16, TT))
         a8 = jnp.broadcast_to(comb[n, LIVE, :], (16, TT))
         c8 = jnp.broadcast_to(comb[n, SRC, :], (16, TT))
+        live = c8 > 0
         l8 = jnp.broadcast_to(comb[n, MAX, :].astype(I32) - cid * BLK, (16, TT))
         for i in range(BLK // 16):
             rows = slice(i * 16, (i + 1) * 16)
             g = jnp.exp(zb[slot, n, rows, :] - m8) * a8
             at = jnp.concatenate([sub + i * 16] * (TT // LANES), axis=1)
             g = g - jnp.where(at == l8, c8, 0.0)
+            if n:
+                g = jnp.where(live, g, 0.0)
             dzb[n % 2, rows, :] = g.astype(BF16)
             part = sum(g[:, cols] for cols in cuts(TT))
             dacc[rows, :] = part if n == 0 else dacc[rows, :] + part
@@ -494,13 +506,11 @@
 
     def step(k, carry):
         slot = lax.rem(k, 2)
-        for cp in loads(k):
-            cp.wait()
+        loads(k, wait)
 
         @pl.when(k < 15)
         def _():
-            for cp in loads(k + 1):
-                cp.start()
+            loads(k + 1, start)
 
         for i in range(4):
             @pl.when(k == i + 8)
@@ -682,7 +692,7 @@
             dwt[:, cols] = mm(hown[...], dub[:, cols], TN)
         i_wr = send(dwt.at[pl.ds(al(other * HD), HD)], wr, sib)
         vect[tp] = jnp.concatenate([jnp.sum(vec[i], **ROWS) for i in range(GB)], axis=0)
-        ids = [send(vect.at[tp], vect.at[tp], at_t(r)) for r in range(1, 8)]
+        ids = [send(vect.at[tp], vect.at[tp], at_t(r)) for r in OTHERS]
         begin("w", flow_w(dwt, i_wr))
         begin("v", flow_v(ids))
         for cols in cuts(D):
@@ -760,7 +770,7 @@
 
     def flow_v(ids):
         yield
-        for r, i in zip(range(1, 8), ids):
+        for r, i in zip(OTHERS, ids):
             got(vect.at[rem8(tp - r)], i)
         vecq[q] = sum(vect[k] for k in range(8))
         ids = share(vecq, q, at_q)
@@ -844,21 +854,22 @@
     ins.append(pltpu.make_async_copy(dwt_hbm, wstage, dsem.at[NCH]))
     outs.append(pltpu.make_async_copy(wstage, dW, esem.at[NCH]))
 
+    per = d.G // NCH
     rows_h = [pltpu.make_async_copy(dh_hbm.at[pl.ds(c * d.NR, d.NR)], dhb.at[pl.ds(c * d.NR, d.NR)], isem.at[c])
               for c in range(NCH)]
-    rows_h.append(pltpu.make_async_copy(col_hbm, colb, isem.at[NCH]))
+    rows_c = pltpu.make_async_copy(col_hbm, colb, ssem.at[1])
 
     def out_copy(g, slot):
         return pltpu.make_async_copy(outb.at[slot], dH.at[pl.ds(g * rows_g, rows_g)], osem.at[slot])
 
-    for cp in rows_h[NCH:] + rows_h[:2] + ins[:2] + rows_h[2:NCH] + ins[2:]:
-        cp.start()
+    rows_c.start()
+    rows_h[0].start()
     for row, ref in ((LAB, g_out), (LIVE, b_out), (SRC, t_out)):
         for i, cols in enumerate(cuts(d.D)):
             ref[slice(i, i + 1), :] = vec_ref[row, cols]
     loss[...] = dbo_ref[16:17, LAB]
     first.wait()
-    rows_h[NCH].wait()
+    rows_c.wait()
 
     def group(g, o):
         oslot = lax.rem(g, NBUF)
@@ -866,10 +877,17 @@
         for j in range(1, GB):
             c = c + cnt[0, g * GB + j]
         o = pl.multiple_of(o, 16)
-        for i in range(NCH):
-            @pl.when(g == i * (d.G // NCH))
+        for i in range(NCH + 1):
+            @pl.when(g == min(i * per, d.G - 1))
             def _(i=i):
-                rows_h[i].wait()
+                if i < NCH:
+                    rows_h[i].wait()
+                if i + 1 < NCH:
+                    rows_h[i + 1].start()
+                ins[i].start()
+                if i:
+                    ins[i - 1].wait()
+                    outs[i - 1].start()
 
         @pl.when(g >= NBUF)
         def _():
@@ -879,18 +897,13 @@
         hot = (src_iota == src).astype(BF16)
         outb[oslot] = mm(hot, dhb[pl.ds(o, d.S), :].astype(BF16), TN).astype(BF16)
         out_copy(g, oslot).start()
-
-        for i, (a, b) in enumerate(zip(ins, outs)):
-            @pl.when(g == min(i, d.G - 1))
-            def _(a=a, b=b):
-                a.wait()
-                b.start()
-
-        return o + ((c + 15) // 16) * 16
+        return o + up16(c)
 
     lax.fori_loop(0, d.G, group, jnp.int32(0))
     for g in range(d.G - NBUF, d.G):
         out_copy(g, g % NBUF).wait()
+    ins[NCH].wait()
+    outs[NCH].start()
     for cp in outs:
         cp.wait()
 
@@ -909,7 +922,7 @@
         scratch_shapes=[
             pltpu.SMEM((GB, d.B), I32), pltpu.VMEM((d.N, LANES), F32), pltpu.VMEM((d.N, d.D), F32),
             pltpu.VMEM((d.VP, d.D), F32), pltpu.VMEM((d.D, d.D), F32), pltpu.VMEM((NBUF, GB * d.L, d.D), BF16),
-            dma((NCH + 1,)), dma((NBUF,)), dma((NCH + 1,)), dma((NCH + 1,)), dma((1,)),
+            dma((NCH,)), dma((NBUF,)), dma((NCH + 1,)), dma((NCH + 1,)), dma((2,)),
         ],
         compiler_params=pltpu.CompilerParams(vmem_limit_bytes=VMEM_MAX),
         name="mlm_finish",
@@ -921,9 +934,9 @@
         d = Dims(hidden.shape, positions.shape, embed.shape)
         bias = jnp.pad(out_bias, (0, d.VP - d.V), constant_values=PAD_BIAS).reshape(-1, LANES)
         bt, gm, be = (v.reshape(-1, LANES) for v in (b_t, gamma, beta))
-        h, t, z, meta, col, e, cnt = forward(d, hidden.reshape(-1, d.D), positions.T, labels.T, weights.T,
+        h, t, z, meta, col, cnt = forward(d, hidden.reshape(-1, d.D), positions.T, labels.T, weights.T,
                                              w_t, bt, gm, be, embed, bias)
-        de, dh, dwt, vec, dbo = train(d, t, h, z, meta, e, w_t, bt, gm, be)
+        de, dh, dwt, vec, dbo = train(d, t, h, z, meta, embed, w_t, bt, gm, be)
         d_hidden, d_embed, d_w, d_gamma, d_beta, d_bt, loss = finish(d, cnt, col, dh, de, dwt, vec, dbo)
         d_bias = dbo[:16, :d.BLK].reshape(-1)[:d.V]
         return (loss.reshape(()), d_hidden.reshape(hidden.shape), d_w, d_bt.reshape(-1), d_gamma.reshape(-1),

time: 224 us -> 228 us (1.018)
  Pallas kernels: 217 us -> 223 us
    pallas_call x1, Pallas kernels: 159 us -> 165 us  [train(): pl.pallas_call(functools.partial(train_kernel, d), out_shape=(sd((d.VP, D...]
where the time goes in v4:
time: 228 us; the launch traced here: 227 us
  Pallas kernels  223 us (98%)
  local copies, waits for them, and re-layouts  2.74 us (1%)
    pallas_call x1, Pallas kernels, train(): pl.pallas_call(functools.partial(train_kernel, d), out_shape=(sd((d.VP, D...  165 us
    pallas_call x1, Pallas kernels, forward(): pl.pallas_call(functools.partial(forward_kernel, d), out_shape=(sd((d.NR,...  32.6 us
    pallas_call x1, Pallas kernels, finish(): pl.pallas_call(functools.partial(finish_kernel, d), out_shape=(sd((d.B *...  25.4 us

profile of v4, /device:TPU:1, one launch (start us, length us, event | category | flops | bytes accessed | tf_op | source)
XLA Modules:
  0.0 226.8 jit_solution(2267934291378793777)
XLA Ops:
  0.6 1.3 pad_bitcast_fusion.bias_ref
  2.0 32.6 %mlm_forward.1 = (bf16[320,768]{1,0:T(8,128)(2,1)}, bf16[2560,768]{1,0:T(8,128)(2,1)}, f32[5,3840,512]{2,1,0:T(8,128)}, f32[5,8,512]{2,1,0:T(8,128)}, f32[2560,128]{1,0:T(8,128)}, /*index=5*/s32[8,128]{1,0:T(8,128)}) custom-call(bf16[16384,768]{1,0:T(8,128)(2,1)} %bitcast.15, s32[20,128]{1,0:T(8,128)} %bitcast.23, s32[20,128]{1,0:T(8,128)} %bitcast.24, ...), custom_call_target="tpu_custom_call" | custom-call | tf_op jit(solution)/shard_map/mlm_forward/pallas_call | solution.py:263
  34.6 165.3 %mlm_train.1 = (f32[3840,768]{1,0:T(8,128)}, f32[2560,768]{1,0:T(8,128)}, f32[768,768]{1,0:T(8,128)}, f32[8,768]{1,0:T(8,128)}, f32[24,256]{1,0:T(8,128)}) custom-call(bf16[2560,768]{1,0:T(8,128)(2,1)} %get-tuple-element.28.t_hbm, bf16[320,768]{1,0:T(8,128)(2,1)} %get-tuple-element.29.h_hbm, f32[5,3840,512]{2,1,0:T(8,128)} %get-tuple-element.30.z_hbm, ...), custom_call_target="tpu_custom_call" | custom-call | tf_op jit(solution)/shard_map/mlm_train/pallas_call | solution.py:823
  199.8 0.7 slice.6
  200.6 0.7 reshape.59
  201.3 25.4 %mlm_finish.1 = (bf16[16384,768]{1,0:T(8,128)(2,1)}, f32[3824,768]{1,0:T(8,128)}, f32[768,768]{1,0:T(8,128)}, f32[6,128]{1,0:T(8,128)}, f32[6,128]{1,0:T(8,128)}, /*index=5*/f32[6,128]{1,0:T(8,128)}, f32[1,1]{1,0:T(1,128)}) custom-call(s32[8,128]{1,0:T(8,128)} %get-tuple-element.26.cnt_hbm, f32[2560,128]{1,0:T(8,128)} %get-tuple-element.27.col_hbm, ...), custom_call_target="tpu_custom_call" | custom-call | tf_op jit(solution)/shard_map/mlm_finish/pallas_call | solution.py:917
